TPU v7x, 32 devices: a whole 2x2x4 slice. The times are simulated.
32 devices in a mesh: row: 4 (over y, x), col: 8 (over z, core).
Axes of the slice: x: 2, y: 2, z: 4, core: 2. Of those that a mesh axis runs over, the one named last changes fastest.
Arguments:
- left_tiles: bfloat16 [2, 32, 256, 256], P(None, 'row', 'col'), may hold values from 0.02 to 3, as said below
- right_tile_store: bfloat16 [32, 24, 256, 256], P('col', 'row'), may hold values from 0.019897461 to 1
- right_index: int32 [32, 24], P('col', 'row'), may hold values from 0 to 7, as said below
- right_count: int32 [32, 4], P('col', 'row'), may hold values from 1 to 6
Outputs:
- inflated: bfloat16 [2, 32, 256, 256], P(None, 'col', 'row')
Inputs may be any that keep to these rules, and one draw needn't show every extreme that they name: `right_index`: for each column block and each row index the 6 slots name distinct contraction blocks; only the first right_count of them are used. `left_tiles`: positive entries.
All inputs are finite; a program needn't handle non-finite values.
Results may differ from a plain program's by a relative error of at most 0.001.
Values may be sent and summed in bfloat16 or wider, within the bound.
No kernel may reach another device: no remote copies, remote signals or barrier semaphores. Data moves between devices by JAX's collectives and lax.ppermute only.
A program may use at most 64 MiB of HBM per device.

v0:
```python
import functools
import jax
import jax.numpy as jnp
from jax import lax
from jax.experimental import pallas as pl
from jax.experimental.pallas import tpu as pltpu
from jax.sharding import PartitionSpec as P


LEVELS = 65280.0
OFFSET = 32640
LOG_STEPS = 256.0
CODE_ROWS = 16
LINE = 4

VMEM = pl.BlockSpec(memory_space=pltpu.VMEM)
SMEM = pl.BlockSpec(memory_space=pltpu.SMEM)


def stage_kernel(right_ref, out_ref, sems):
    copies = [
        pltpu.make_async_copy(right_ref.at[j], out_ref.at[j], sems.at[j])
        for j in range(right_ref.shape[0])
    ]
    for copy in copies:
        copy.start()
    for copy in copies:
        copy.wait()


def far_half(half):
    chip = lax.axis_index("col") >> 1
    return jnp.where(lax.axis_index("row") == chip ^ (LINE - 1), 1 - half, half)


def turned(k, half):
    if half is None or k > 2:
        return k
    return jnp.where(lax.axis_index("col") & 1 == 0, k, 3 - k)


def product_kernel(n_row, spans, half, index_ref, count_ref, *refs):
    n_block = len(refs) - n_row - 3
    blocks, right_ref, own_ref = refs[:n_block], refs[n_block], refs[n_block + 1]
    sent_refs = refs[n_block + 2 : n_block + 1 + n_row]
    left, partial = refs[-2:]
    column_blocks, slots, tile, _ = right_ref.shape
    kept, height = left.shape[0] - 1, left.shape[1]
    part = height // n_row // len(spans[0])
    row = lax.axis_index("row")

    def rows_of(owner, at):
        return pl.ds(pl.multiple_of((at * n_row + owner) * part, part), part)

    def block_of(span):
        at, a = span
        return blocks[at] if a is None else blocks[at].at[a]

    if half is None:
        left[:kept] = block_of(spans[0][0])[...]
    else:
        core, chip = lax.axis_index("col") & 1, lax.axis_index("col") >> 1
        ends = (chip == 0) | (chip == LINE - 1)
        first, last = core == 0, core == 1
        placed = [(half, 0, first), (1 - half, 0, last)]
        placed += [(2 + half, 1, first), (3 - half, 1, last), (4, 2, first), (5, 2, last)]
        if half:
            inner = jnp.logical_not(ends)
            placed += [(5, 3, first & inner), (4, 3, last & inner)]
            placed += [(7, 3, first & ends), (6, 3, last & ends)]
        else:
            placed += [(5, 3, first), (4, 3, last)]
        for role, k, wanted in placed:

            def fill(role=role, k=k):
                for at, span in enumerate(spans[role]):
                    left[:kept, rows_of(chip ^ k, at), :] = block_of(span)[...]

            pl.when(wanted)(fill)
    left[kept] = jnp.zeros(left.shape[1:], left.dtype)
    lines = lax.broadcasted_iota(jnp.int32, (CODE_ROWS, tile), 0)
    codes = jnp.zeros((CODE_ROWS, tile), jnp.int32)
    count = len(spans[0])
    for j in range(column_blocks):
        total = None
        for q in range(slots):
            picked = jnp.where(q < count_ref[j], index_ref[j, q], kept)
            term = jnp.dot(left[picked], right_ref[j, q], preferred_element_type=jnp.float32)
            total = term if total is None else total + term
        partial[...] = total
        top = jnp.max(total, axis=0, keepdims=True)
        code = jnp.floor(jnp.log2(top) * LOG_STEPS).astype(jnp.int32) + 2
        grow = LEVELS * jnp.exp2(code.astype(jnp.float32) * (-1.0 / LOG_STEPS))
        codes = jnp.where(lines == j, code, codes)
        for at in range(count):
            own_ref[j, at * part : (at + 1) * part, :] = partial[rows_of(row, at), :]
            for k in range(1, n_row):
                coded = (partial[rows_of(row ^ turned(k, half), at), :] * grow + 0.5).astype(jnp.int32) - OFFSET
                first = (j * count + at) * part
                sent_refs[k - 1][first : first + part, :] = coded.astype(jnp.int16)
    for sent in sent_refs:
        sent[column_blocks * count * part :, :] = codes.astype(jnp.int16)


def reduce_kernel(n_row, has_before, *refs):
    got_refs = refs[: n_row - 1]
    own_ref = refs[n_row - 1]
    before_ref = refs[n_row] if has_before else None
    squared_ref, sums_ref = refs[-2:]
    column_blocks, part, _ = own_ref.shape
    shrinks = []
    for got in got_refs:
        code = got[column_blocks * part :, :].astype(jnp.int32)
        shrinks.append(jnp.exp2(code.astype(jnp.float32) * (1.0 / LOG_STEPS)) * (1.0 / LEVELS))
    for j in range(column_blocks):
        total = own_ref[j]
        for got, shrink in zip(got_refs, shrinks):
            coded = got[j * part : (j + 1) * part, :].astype(jnp.int32) + OFFSET
            total = total + coded.astype(jnp.float32) * shrink[j : j + 1]
        squared = total * total
        squared_ref[j] = squared
        sums = jnp.sum(squared, axis=0, keepdims=True)
        if has_before:
            sums = sums + before_ref[j : j + 1]
        sums_ref[j : j + 1] = sums


def scale_kernel(chunks, n_row, *refs):
    squared_refs = refs[: len(chunks)]
    sums_refs = refs[len(chunks) : len(chunks) + n_row]
    out_ref = refs[-1]
    windows, column_blocks, _, tile = out_ref.shape
    total = sums_refs[0][...]
    for other in sums_refs[1:]:
        total = total + other[...]
    scale = (windows * tile) / total
    for (picked, half), squared in zip(chunks, squared_refs):
        rows = squared.shape[1] // len(picked)
        for at, a in enumerate(picked):
            for j in range(column_blocks):
                value = squared[j, at * rows : (at + 1) * rows, :] * scale[j : j + 1]
                first = 0 if half is None else pl.multiple_of(far_half(half) * rows, rows)
                out_ref[a, j, pl.ds(first, rows), :] = value.astype(out_ref.dtype)


def move(x, axis, pairs, turn=0):
    return lax.ppermute(x, axis, pairs[turn:] + pairs[:turn])


def row_pairs(n_row, n_col, k, half):
    pairs = []
    for i in range(n_row * n_col):
        row, col = i // n_col, i % n_col
        peer = 3 - k if half is not None and k < 3 and col & 1 else k
        pairs.append((i, (row ^ peer) * n_col + col))
    return pairs


def limits(mib):
    return pltpu.CompilerParams(vmem_limit_bytes=mib << 20)


def is_line(n_row, n_col):
    return n_row == LINE and n_col == 2 * LINE


def gather_line(left_tiles, n_col):
    windows = left_tiles.shape[0]
    swap = [(i, i ^ 1) for i in range(n_col)]
    across = [(i, i ^ (4 if i & 1 == 0 else 6)) for i in range(n_col)]
    inner = [p if p[0] & 1 == 0 or 2 <= p[0] < n_col - 2 else (p[0], p[0]) for p in across]
    beside = move(left_tiles, "col", [(i, i ^ 2) for i in range(n_col)])
    own = move(left_tiles, "col", across)
    pair = move(left_tiles, "col", swap, 1)
    other = move(pair, "col", inner)
    relay = move(own, "col", [(2, 1), (n_col - 4, n_col - 1)])
    near_beside = move(beside, "col", swap, 2)
    near_own = move(own, "col", swap, 3)
    near_other = move(other, "col", swap, 4)
    near_relay = move(relay, "col", swap, 5)
    base = [left_tiles, pair, beside, near_beside]
    chunks, gathered = [], []
    for half, more in enumerate(([own, near_own], [other, near_other, relay, near_relay])):
        arrays = base + more
        chunks.append((tuple(range(windows)), half))
        gathered.append((arrays, tuple(tuple((at, a) for a in range(windows)) for at in range(len(arrays)))))
    return chunks, gathered


def shards(n_row, n_col, left_tiles, right, right_index, right_count):
    windows, kept, _, tile = left_tiles.shape
    column_blocks, slots = right.shape[:2]
    right_count = right_count.reshape(-1)

    if is_line(n_row, n_col):
        chunks, gathered = gather_line(left_tiles, n_col)
        height = tile // 2
    else:
        whole = lax.all_gather(left_tiles, "col", axis=2, tiled=True)
        chunks = [((a,), None) for a in range(windows)]
        gathered = [([whole], (((0, a),),)) for a in range(windows)]
        height = tile

    staged = pl.pallas_call(
        stage_kernel,
        out_shape=jax.ShapeDtypeStruct(right.shape, right.dtype),
        in_specs=[pl.BlockSpec(memory_space=pltpu.HBM)],
        out_specs=VMEM,
        scratch_shapes=[pltpu.SemaphoreType.DMA((column_blocks,))],
        compiler_params=limits(8),
        name="stage",
    )(right)
    exchanged = []
    for at, ((picked, half), (arrays, spans)) in enumerate(zip(chunks, gathered)):
        tall = height * len(picked)
        part = tall // n_row
        own, *sent = pl.pallas_call(
            functools.partial(product_kernel, n_row, spans, half),
            out_shape=[jax.ShapeDtypeStruct((column_blocks, part, tile), jnp.float32)]
            + [jax.ShapeDtypeStruct((column_blocks * part + CODE_ROWS, tile), jnp.int16)] * (n_row - 1),
            in_specs=[SMEM] * 2 + [VMEM] * (len(arrays) + 1),
            out_specs=[VMEM] * n_row,
            scratch_shapes=[
                pltpu.VMEM((kept + 1, tall, tile), left_tiles.dtype),
                pltpu.VMEM((tall, tile), jnp.float32),
            ],
            cost_estimate=pl.CostEstimate(
                flops=2 * column_blocks * slots * tall * tile**2,
                bytes_accessed=right.size * 2,
                transcendentals=0,
            ),
            compiler_params=limits(16),
            name="product",
        )(right_index, right_count, *arrays, staged)
        got = [
            move(x, ("row", "col"), row_pairs(n_row, n_col, k, half), at)
            for k, x in enumerate(sent, 1)
        ]
        exchanged.append((own, got))
    squared, sums = [], None
    for at, (own, got) in enumerate(exchanged):
        square, sums = pl.pallas_call(
            functools.partial(reduce_kernel, n_row, at > 0),
            out_shape=[
                jax.ShapeDtypeStruct(own.shape, jnp.float32),
                jax.ShapeDtypeStruct((column_blocks, tile), jnp.float32),
            ],
            in_specs=[VMEM] * (n_row + (at > 0)),
            out_specs=[VMEM] * 2,
            compiler_params=limits(8),
            name="reduce",
        )(*got, own, *([sums] if at else []))
        squared.append(square)
    others = [move(sums, "row", [(i, i ^ k) for i in range(n_row)]) for k in range(1, n_row)]
    return pl.pallas_call(
        functools.partial(scale_kernel, chunks, n_row),
        out_shape=jax.ShapeDtypeStruct((windows, column_blocks, tile // n_row, tile), jnp.bfloat16),
        in_specs=[VMEM] * (len(chunks) + n_row),
        out_specs=VMEM,
        compiler_params=limits(8),
        name="scale",
    )(*squared, sums, *others)


def solution(mesh):
    in_specs = (
        P(None, "row", "col", None),
        P("col", "row", None, None),
        P("col", "row"),
        P("col", "row"),
    )
    out_specs = P(None, "col", "row", None)
    n_row, n_col = mesh.shape["row"], mesh.shape["col"]

    def body(*args):
        return shards(n_row, n_col, *args)

    return jax.shard_map(body, mesh=mesh, in_specs=in_specs, out_specs=out_specs, check_vma=False)
```

profile of v0, /device:TPU:0, one launch (start us, length us, event | category | flops | bytes accessed | tf_op | source)
XLA Modules:
  0.0 57.2 jit_solution(18078414805057461848)
XLA Ops:
  0.0 4.1 %collective-permute-start.3 = (bf16[2,8,32,256]{3,2,1,0:T(8,128)(2,1)}, bf16[2,8,32,256]{3,2,1,0:T(8,128)(2,1)S(1)}, u32[]{:S(2)}, u32[]{:S(2)}) collective-permute-start(bf16[2,8,32,256]{3,2,1,0:T(8,128)(2,1)} %refs_0_.3), channel_id=1, source_target_pairs={{0,4},{1,7},{2,6},{3,5},{4,0},{5,3},{6,2},{7,1},{8,12},{9,15},{10,... | collective-permute-start | bytes 786440 | tf_op jit(solution)/shard_map/ppermute | solution.py:147
  4.1 0.6 collective-permute-start
  4.6 1.0 %collective-permute-start.1 = (bf16[2,8,32,256]{3,2,1,0:T(8,128)(2,1)}, bf16[2,8,32,256]{3,2,1,0:T(8,128)(2,1)S(1)}, u32[]{:S(2)}, u32[]{:S(2)}) collective-permute-start(bf16[2,8,32,256]{3,2,1,0:T(8,128)(2,1)} %refs_0_.3), channel_id=1, source_target_pairs={{0,2},{1,3},{2,0},{3,1},{4,6},{5,7},{6,4},{7,5},{8,10},{9,11},{10,... | collective-permute-start | bytes 786440 | tf_op jit(solution)/shard_map/ppermute | solution.py:147
  5.6 10.8 %collective-permute-done.3.refs_4_ = bf16[2,8,32,256]{3,2,1,0:T(8,128)(2,1)S(1)} collective-permute-done((bf16[2,8,32,256]{3,2,1,0:T(8,128)(2,1)}, bf16[2,8,32,256]{3,2,1,0:T(8,128)(2,1)S(1)}, u32[]{:S(2)}, u32[]{:S(2)}) %collective-permute-start.3) | collective-permute-done | bytes 262176 | tf_op jit(solution)/shard_map/ppermute | solution.py:147
  16.5 0.7 %collective-permute-start.10 = (bf16[2,8,32,256]{3,2,1,0:T(8,128)(2,1)S(1)}, bf16[2,8,32,256]{3,2,1,0:T(8,128)(2,1)S(1)}, u32[]{:S(2)}, u32[]{:S(2)}) collective-permute-start(bf16[2,8,32,256]{3,2,1,0:T(8,128)(2,1)S(1)} %collective-permute-done.3.refs_4_), channel_id=1, source_target_pairs={{2,1},{4,7},{10,9},{12,15},{18,17},{20,23},{26,25},{28,31}} | collective-permute-start | bytes 786440 | tf_op jit(solution)/shard_map/ppermute | solution.py:147
  17.1 2.1 %collective-permute-start.8 = (bf16[2,8,32,256]{3,2,1,0:T(8,128)(2,1)S(1)}, bf16[2,8,32,256]{3,2,1,0:T(8,128)(2,1)S(1)}, u32[]{:S(2)}, u32[]{:S(2)}) collective-permute-start(bf16[2,8,32,256]{3,2,1,0:T(8,128)(2,1)S(1)} %collective-permute-done.refs_1_), channel_id=1, source_target_pairs={{0,4},{1,1},{2,6},{3,5},{4,0},{5,3},{6,2},{7,7},{8,12},{9,9},{10,1... | collective-permute-start | bytes 786440 | tf_op jit(solution)/shard_map/ppermute | solution.py:147
  19.3 0.5 collective-permute-start.4
  19.8 1.7 %collective-permute-start.11 = (bf16[2,8,32,256]{3,2,1,0:T(8,128)(2,1)S(1)}, bf16[2,8,32,256]{3,2,1,0:T(8,128)(2,1)S(1)}, u32[]{:S(2)}, u32[]{:S(2)}) collective-permute-start(bf16[2,8,32,256]{3,2,1,0:T(8,128)(2,1)S(1)} %collective-permute-done.10.refs_6_), channel_id=1, source_target_pairs={{5,4},{6,7},{7,6},{0,1},{1,0},{2,3},{3,2},{4,5},{13,12},{14,15},{1... | collective-permute-start | bytes 786440 | tf_op jit(solution)/shard_map/ppermute | solution.py:147
  21.6 7.8 %collective-permute-done.8.refs_4_ = bf16[2,8,32,256]{3,2,1,0:T(8,128)(2,1)S(1)} collective-permute-done((bf16[2,8,32,256]{3,2,1,0:T(8,128)(2,1)S(1)}, bf16[2,8,32,256]{3,2,1,0:T(8,128)(2,1)S(1)}, u32[]{:S(2)}, u32[]{:S(2)}) %collective-permute-start.8) | collective-permute-done | bytes 262176 | tf_op jit(solution)/shard_map/ppermute | solution.py:147
  29.4 1.9 %copy-done = bf16[4,6,256,256]{3,2,1,0:T(8,128)(2,1)S(1)} copy-done((bf16[4,6,256,256]{3,2,1,0:T(8,128)(2,1)S(1)}, bf16[4,6,256,256]{3,2,1,0:T(8,128)(2,1)}, u32[]{:S(2)}) %copy-start) | copy-done | bytes 3145752
  31.3 0.3 stage.1.refs_6_.refs_8_
  31.6 0.7 %copy-done.1 = bf16[2,8,32,256]{3,2,1,0:T(8,128)(2,1)S(1)} copy-done((bf16[2,8,32,256]{3,2,1,0:T(8,128)(2,1)S(1)}, bf16[2,8,32,256]{3,2,1,0:T(8,128)(2,1)}, u32[]{:S(2)}) %copy-start.1) | copy-done | bytes 262168
  32.2 1.8 %product.2 = (f32[4,64,256]{2,1,0:T(8,128)S(1)}, s16[272,256]{1,0:T(8,128)(2,1)S(1)}, s16[272,256]{1,0:T(8,128)(2,1)S(1)}, s16[272,256]{1,0:T(8,128)(2,1)S(1)}) custom-call(s32[4,6]{1,0:T(4,128)S(1)} %copy-done.2, s32[4]{0:T(128)S(1)} %bitcast.1, bf16[2,8,32,256]{3,2,1,0:T(8,128)(2,1)S(1)} %copy-done.1, ...), custom_call_target="tpu_custom_call" | custom-call | flops 805306368 | bytes 3145728 | tf_op jit(solution)/shard_map/product/pallas_call | solution.py:217
  34.1 1.3 %collective-permute-start.5 = (s16[272,256]{1,0:T(8,128)(2,1)S(1)}, s16[272,256]{1,0:T(8,128)(2,1)S(1)}, u32[]{:S(2)}, u32[]{:S(2)}) collective-permute-start(s16[272,256]{1,0:T(8,128)(2,1)S(1)} %get-tuple-element.17), channel_id=1, source_target_pairs={{0,8},{1,17},{2,10},{3,19},{4,12},{5,21},{6,14},{7,23},{8,0},{9,25... | collective-permute-start | bytes 417800 | tf_op jit(solution)/shard_map/ppermute | solution.py:147
  35.4 1.5 %collective-permute-start.6 = (s16[272,256]{1,0:T(8,128)(2,1)S(1)}, s16[272,256]{1,0:T(8,128)(2,1)S(1)}, u32[]{:S(2)}, u32[]{:S(2)}) collective-permute-start(s16[272,256]{1,0:T(8,128)(2,1)S(1)} %get-tuple-element.18), channel_id=1, source_target_pairs={{0,16},{1,9},{2,18},{3,11},{4,20},{5,13},{6,22},{7,15},{8,24},{9,1... | collective-permute-start | bytes 417800 | tf_op jit(solution)/shard_map/ppermute | solution.py:147
  36.9 0.7 %collective-permute-start.7 = (s16[272,256]{1,0:T(8,128)(2,1)S(1)}, s16[272,256]{1,0:T(8,128)(2,1)S(1)}, u32[]{:S(2)}, u32[]{:S(2)}) collective-permute-start(s16[272,256]{1,0:T(8,128)(2,1)S(1)} %get-tuple-element.19), channel_id=1, source_target_pairs={{0,24},{1,25},{2,26},{3,27},{4,28},{5,29},{6,30},{7,31},{8,16},{9,... | collective-permute-start | bytes 417800 | tf_op jit(solution)/shard_map/ppermute | solution.py:147
  37.6 1.8 %product.3 = (f32[4,64,256]{2,1,0:T(8,128)S(1)}, s16[272,256]{1,0:T(8,128)(2,1)S(1)}, s16[272,256]{1,0:T(8,128)(2,1)S(1)}, s16[272,256]{1,0:T(8,128)(2,1)S(1)}) custom-call(s32[4,6]{1,0:T(4,128)S(1)} %copy-done.2, s32[4]{0:T(128)S(1)} %bitcast.2, bf16[2,8,32,256]{3,2,1,0:T(8,128)(2,1)S(1)} %copy-done.1, ...), custom_call_target="tpu_custom_call" | custom-call | flops 805306368 | bytes 3145728 | tf_op jit(solution)/shard_map/product/pallas_call | solution.py:217
  39.4 1.3 %collective-permute-start.12 = (s16[272,256]{1,0:T(8,128)(2,1)S(1)}, s16[272,256]{1,0:T(8,128)(2,1)S(1)}, u32[]{:S(2)}, u32[]{:S(2)}) collective-permute-start(s16[272,256]{1,0:T(8,128)(2,1)S(1)} %get-tuple-element.22), channel_id=1, source_target_pairs={{1,17},{2,10},{3,19},{4,12},{5,21},{6,14},{7,23},{8,0},{9,25},{10,... | collective-permute-start | bytes 417800 | tf_op jit(solution)/shard_map/ppermute | solution.py:147
  40.7 1.5 %collective-permute-start.13 = (s16[272,256]{1,0:T(8,128)(2,1)S(1)}, s16[272,256]{1,0:T(8,128)(2,1)S(1)}, u32[]{:S(2)}, u32[]{:S(2)}) collective-permute-start(s16[272,256]{1,0:T(8,128)(2,1)S(1)} %get-tuple-element.23), channel_id=1, source_target_pairs={{1,9},{2,18},{3,11},{4,20},{5,13},{6,22},{7,15},{8,24},{9,1},{10,2... | collective-permute-start | bytes 417800 | tf_op jit(solution)/shard_map/ppermute | solution.py:147
  42.3 0.7 %collective-permute-start.14 = (s16[272,256]{1,0:T(8,128)(2,1)S(1)}, s16[272,256]{1,0:T(8,128)(2,1)S(1)}, u32[]{:S(2)}, u32[]{:S(2)}) collective-permute-start(s16[272,256]{1,0:T(8,128)(2,1)S(1)} %get-tuple-element.24), channel_id=1, source_target_pairs={{1,25},{2,26},{3,27},{4,28},{5,29},{6,30},{7,31},{8,16},{9,17},{10... | collective-permute-start | bytes 417800 | tf_op jit(solution)/shard_map/ppermute | solution.py:147
  43.0 1.4 %collective-permute-done.7.refs_2_ = s16[272,256]{1,0:T(8,128)(2,1)S(1)} collective-permute-done((s16[272,256]{1,0:T(8,128)(2,1)S(1)}, s16[272,256]{1,0:T(8,128)(2,1)S(1)}, u32[]{:S(2)}, u32[]{:S(2)}) %collective-permute-start.7) | collective-permute-done | bytes 139296 | tf_op jit(solution)/shard_map/ppermute | solution.py:147
  44.4 0.2 reduce.2
  44.6 1.8 %collective-permute-done.12.refs_0_ = s16[272,256]{1,0:T(8,128)(2,1)S(1)} collective-permute-done((s16[272,256]{1,0:T(8,128)(2,1)S(1)}, s16[272,256]{1,0:T(8,128)(2,1)S(1)}, u32[]{:S(2)}, u32[]{:S(2)}) %collective-permute-start.12) | collective-permute-done | bytes 139296 | tf_op jit(solution)/shard_map/ppermute | solution.py:147
  46.4 1.0 %collective-permute-done.13.refs_1_ = s16[272,256]{1,0:T(8,128)(2,1)S(1)} collective-permute-done((s16[272,256]{1,0:T(8,128)(2,1)S(1)}, s16[272,256]{1,0:T(8,128)(2,1)S(1)}, u32[]{:S(2)}, u32[]{:S(2)}) %collective-permute-start.13) | collective-permute-done | bytes 139296 | tf_op jit(solution)/shard_map/ppermute | solution.py:147
  47.3 3.0 %collective-permute-done.14.refs_2_ = s16[272,256]{1,0:T(8,128)(2,1)S(1)} collective-permute-done((s16[272,256]{1,0:T(8,128)(2,1)S(1)}, s16[272,256]{1,0:T(8,128)(2,1)S(1)}, u32[]{:S(2)}, u32[]{:S(2)}) %collective-permute-start.14) | collective-permute-done | bytes 139296 | tf_op jit(solution)/shard_map/ppermute | solution.py:147
  50.3 0.2 reduce.3
  50.5 1.3 %collective-permute-start.15 = (f32[4,256]{1,0:T(4,128)S(1)}, f32[4,256]{1,0:T(4,128)S(1)}, u32[]{:S(2)}, u32[]{:S(2)}) collective-permute-start(f32[4,256]{1,0:T(4,128)S(1)} %get-tuple-element.28.refs_2_), channel_id=1, source_target_pairs={{0,8},{8,0},{16,24},{24,16},{1,9},{9,1},{17,25},{25,17},{2,10},{10... | collective-permute-start | bytes 12296 | tf_op jit(solution)/shard_map/ppermute | solution.py:147
  52.0 2.1 %collective-permute-start.17 = (f32[4,256]{1,0:T(4,128)S(1)}, f32[4,256]{1,0:T(4,128)S(1)}, u32[]{:S(2)}, u32[]{:S(2)}) collective-permute-start(f32[4,256]{1,0:T(4,128)S(1)} %get-tuple-element.28.refs_2_), channel_id=1, source_target_pairs={{0,24},{8,16},{16,8},{24,0},{1,25},{9,17},{17,9},{25,1},{2,26},{10... | collective-permute-start | bytes 12296 | tf_op jit(solution)/shard_map/ppermute | solution.py:147
  54.1 0.1 collective-permute-done.15.refs_3_
  54.2 1.3 %collective-permute-done.16.refs_4_ = f32[4,256]{1,0:T(4,128)S(1)} collective-permute-done((f32[4,256]{1,0:T(4,128)S(1)}, f32[4,256]{1,0:T(4,128)S(1)}, u32[]{:S(2)}, u32[]{:S(2)}) %collective-permute-start.16) | collective-permute-done | bytes 4128 | tf_op jit(solution)/shard_map/ppermute | solution.py:147
  55.5 1.0 %collective-permute-done.17.refs_5_ = f32[4,256]{1,0:T(4,128)S(1)} collective-permute-done((f32[4,256]{1,0:T(4,128)S(1)}, f32[4,256]{1,0:T(4,128)S(1)}, u32[]{:S(2)}, u32[]{:S(2)}) %collective-permute-start.17) | collective-permute-done | bytes 4128 | tf_op jit(solution)/shard_map/ppermute | solution.py:147
  56.5 0.7 %scale.1 = bf16[2,4,64,256]{3,2,1,0:T(8,128)(2,1)} custom-call(f32[4,64,256]{2,1,0:T(8,128)S(1)} %get-tuple-element.21.refs_0_, f32[4,64,256]{2,1,0:T(8,128)S(1)} %get-tuple-element.27.refs_1_, f32[4,256]{1,0:T(4,128)S(1)} %get-tuple-element.28.refs_2_, f32[4,256]{1,0:T(4,128)S(1)} %collective-permute-done.15.refs_3_, ...), custom_call_target="tpu_custom_call" | custom-call | tf_op jit(solution)/shard_map/scale/pallas_call | solution.py:255
  (18 shorter events, 0.2 us)
Async XLA Ops:
  0.0 16.5 %collective-permute-start.3 = (bf16[2,8,32,256]{3,2,1,0:T(8,128)(2,1)}, bf16[2,8,32,256]{3,2,1,0:T(8,128)(2,1)S(1)}, u32[]{:S(2)}, u32[]{:S(2)}) collective-permute-start(bf16[2,8,32,256]{3,2,1,0:T(8,128)(2,1)} %refs_0_.3), channel_id=1, source_target_pairs={{0,4},{1,7},{2,6},{3,5},{4,0},{5,3},{6,2},{7,1},{8,12},{9,15},{10,... | collective-permute-start | bytes 786440 | tf_op jit(solution)/shard_map/ppermute | solution.py:147
  4.1 13.1 %collective-permute-start = (bf16[2,8,32,256]{3,2,1,0:T(8,128)(2,1)}, bf16[2,8,32,256]{3,2,1,0:T(8,128)(2,1)S(1)}, u32[]{:S(2)}, u32[]{:S(2)}) collective-permute-start(bf16[2,8,32,256]{3,2,1,0:T(8,128)(2,1)} %refs_0_.3), channel_id=1, source_target_pairs={{1,0},{2,3},{3,2},{4,5},{5,4},{6,7},{7,6},{0,1},{9,8},{10,11},{11,... | collective-permute-start | bytes 786440 | tf_op jit(solution)/shard_map/ppermute | solution.py:147
  4.6 14.6 %collective-permute-start.1 = (bf16[2,8,32,256]{3,2,1,0:T(8,128)(2,1)}, bf16[2,8,32,256]{3,2,1,0:T(8,128)(2,1)S(1)}, u32[]{:S(2)}, u32[]{:S(2)}) collective-permute-start(bf16[2,8,32,256]{3,2,1,0:T(8,128)(2,1)} %refs_0_.3), channel_id=1, source_target_pairs={{0,2},{1,3},{2,0},{3,1},{4,6},{5,7},{6,4},{7,5},{8,10},{9,11},{10,... | collective-permute-start | bytes 786440 | tf_op jit(solution)/shard_map/ppermute | solution.py:147
  16.5 3.4 %collective-permute-start.10 = (bf16[2,8,32,256]{3,2,1,0:T(8,128)(2,1)S(1)}, bf16[2,8,32,256]{3,2,1,0:T(8,128)(2,1)S(1)}, u32[]{:S(2)}, u32[]{:S(2)}) collective-permute-start(bf16[2,8,32,256]{3,2,1,0:T(8,128)(2,1)S(1)} %collective-permute-done.3.refs_4_), channel_id=1, source_target_pairs={{2,1},{4,7},{10,9},{12,15},{18,17},{20,23},{26,25},{28,31}} | collective-permute-start | bytes 786440 | tf_op jit(solution)/shard_map/ppermute | solution.py:147
  17.1 12.2 %collective-permute-start.8 = (bf16[2,8,32,256]{3,2,1,0:T(8,128)(2,1)S(1)}, bf16[2,8,32,256]{3,2,1,0:T(8,128)(2,1)S(1)}, u32[]{:S(2)}, u32[]{:S(2)}) collective-permute-start(bf16[2,8,32,256]{3,2,1,0:T(8,128)(2,1)S(1)} %collective-permute-done.refs_1_), channel_id=1, source_target_pairs={{0,4},{1,1},{2,6},{3,5},{4,0},{5,3},{6,2},{7,7},{8,12},{9,9},{10,1... | collective-permute-start | bytes 786440 | tf_op jit(solution)/shard_map/ppermute | solution.py:147
  19.3 12.3 %collective-permute-start.2 = (bf16[2,8,32,256]{3,2,1,0:T(8,128)(2,1)S(1)}, bf16[2,8,32,256]{3,2,1,0:T(8,128)(2,1)S(1)}, u32[]{:S(2)}, u32[]{:S(2)}) collective-permute-start(bf16[2,8,32,256]{3,2,1,0:T(8,128)(2,1)S(1)} %collective-permute-done.1.refs_2_), channel_id=1, source_target_pairs={{2,3},{3,2},{4,5},{5,4},{6,7},{7,6},{0,1},{1,0},{10,11},{11,10},{1... | collective-permute-start | bytes 786440 | tf_op jit(solution)/shard_map/ppermute | solution.py:147
  19.3 12.2 %collective-permute-start.4 = (bf16[2,8,32,256]{3,2,1,0:T(8,128)(2,1)S(1)}, bf16[2,8,32,256]{3,2,1,0:T(8,128)(2,1)S(1)}, u32[]{:S(2)}, u32[]{:S(2)}) collective-permute-start(bf16[2,8,32,256]{3,2,1,0:T(8,128)(2,1)S(1)} %collective-permute-done.3.refs_4_), channel_id=1, source_target_pairs={{3,2},{4,5},{5,4},{6,7},{7,6},{0,1},{1,0},{2,3},{11,10},{12,13},{1... | collective-permute-start | bytes 786440 | tf_op jit(solution)/shard_map/ppermute | solution.py:147
  19.8 17.8 %collective-permute-start.11 = (bf16[2,8,32,256]{3,2,1,0:T(8,128)(2,1)S(1)}, bf16[2,8,32,256]{3,2,1,0:T(8,128)(2,1)S(1)}, u32[]{:S(2)}, u32[]{:S(2)}) collective-permute-start(bf16[2,8,32,256]{3,2,1,0:T(8,128)(2,1)S(1)} %collective-permute-done.10.refs_6_), channel_id=1, source_target_pairs={{5,4},{6,7},{7,6},{0,1},{1,0},{2,3},{3,2},{4,5},{13,12},{14,15},{1... | collective-permute-start | bytes 786440 | tf_op jit(solution)/shard_map/ppermute | solution.py:147
  29.4 8.2 %collective-permute-start.9 = (bf16[2,8,32,256]{3,2,1,0:T(8,128)(2,1)S(1)}, bf16[2,8,32,256]{3,2,1,0:T(8,128)(2,1)S(1)}, u32[]{:S(2)}, u32[]{:S(2)}) collective-permute-start(bf16[2,8,32,256]{3,2,1,0:T(8,128)(2,1)S(1)} %collective-permute-done.8.refs_4_), channel_id=1, source_target_pairs={{4,5},{5,4},{6,7},{7,6},{0,1},{1,0},{2,3},{3,2},{12,13},{13,12},{1... | collective-permute-start | bytes 786440 | tf_op jit(solution)/shard_map/ppermute | solution.py:147
  29.4 1.9 %copy-start = (bf16[4,6,256,256]{3,2,1,0:T(8,128)(2,1)S(1)}, bf16[4,6,256,256]{3,2,1,0:T(8,128)(2,1)}, u32[]{:S(2)}) copy-start(bf16[4,6,256,256]{3,2,1,0:T(8,128)(2,1)} %right_ref.1) | copy-start | bytes 9437188
  31.3 0.9 %copy-start.1 = (bf16[2,8,32,256]{3,2,1,0:T(8,128)(2,1)S(1)}, bf16[2,8,32,256]{3,2,1,0:T(8,128)(2,1)}, u32[]{:S(2)}) copy-start(bf16[2,8,32,256]{3,2,1,0:T(8,128)(2,1)} %refs_0_.3) | copy-start | bytes 786436
  31.3 1.0 %copy-start.2 = (s32[4,6]{1,0:T(4,128)S(1)}, s32[4,6]{1,0:T(4,128)}, u32[]{:S(2)}) copy-start(s32[4,6]{1,0:T(4,128)} %index_ref.3) | copy-start | bytes 292
  31.3 1.0 %copy-start.3 = (s32[4,1]{0,1:T(1,128)S(1)}, s32[4,1]{0,1:T(1,128)}, u32[]{:S(2)}) copy-start(s32[4,1]{0,1:T(1,128)} %param.7) | copy-start | bytes 52
  34.1 8.2 %collective-permute-start.5 = (s16[272,256]{1,0:T(8,128)(2,1)S(1)}, s16[272,256]{1,0:T(8,128)(2,1)S(1)}, u32[]{:S(2)}, u32[]{:S(2)}) collective-permute-start(s16[272,256]{1,0:T(8,128)(2,1)S(1)} %get-tuple-element.17), channel_id=1, source_target_pairs={{0,8},{1,17},{2,10},{3,19},{4,12},{5,21},{6,14},{7,23},{8,0},{9,25... | collective-permute-start | bytes 417800 | tf_op jit(solution)/shard_map/ppermute | solution.py:147
  35.4 7.7 %collective-permute-start.6 = (s16[272,256]{1,0:T(8,128)(2,1)S(1)}, s16[272,256]{1,0:T(8,128)(2,1)S(1)}, u32[]{:S(2)}, u32[]{:S(2)}) collective-permute-start(s16[272,256]{1,0:T(8,128)(2,1)S(1)} %get-tuple-element.18), channel_id=1, source_target_pairs={{0,16},{1,9},{2,18},{3,11},{4,20},{5,13},{6,22},{7,15},{8,24},{9,1... | collective-permute-start | bytes 417800 | tf_op jit(solution)/shard_map/ppermute | solution.py:147
  36.9 7.6 %collective-permute-start.7 = (s16[272,256]{1,0:T(8,128)(2,1)S(1)}, s16[272,256]{1,0:T(8,128)(2,1)S(1)}, u32[]{:S(2)}, u32[]{:S(2)}) collective-permute-start(s16[272,256]{1,0:T(8,128)(2,1)S(1)} %get-tuple-element.19), channel_id=1, source_target_pairs={{0,24},{1,25},{2,26},{3,27},{4,28},{5,29},{6,30},{7,31},{8,16},{9,... | collective-permute-start | bytes 417800 | tf_op jit(solution)/shard_map/ppermute | solution.py:147
  39.4 6.9 %collective-permute-start.12 = (s16[272,256]{1,0:T(8,128)(2,1)S(1)}, s16[272,256]{1,0:T(8,128)(2,1)S(1)}, u32[]{:S(2)}, u32[]{:S(2)}) collective-permute-start(s16[272,256]{1,0:T(8,128)(2,1)S(1)} %get-tuple-element.22), channel_id=1, source_target_pairs={{1,17},{2,10},{3,19},{4,12},{5,21},{6,14},{7,23},{8,0},{9,25},{10,... | collective-permute-start | bytes 417800 | tf_op jit(solution)/shard_map/ppermute | solution.py:147
  40.7 6.6 %collective-permute-start.13 = (s16[272,256]{1,0:T(8,128)(2,1)S(1)}, s16[272,256]{1,0:T(8,128)(2,1)S(1)}, u32[]{:S(2)}, u32[]{:S(2)}) collective-permute-start(s16[272,256]{1,0:T(8,128)(2,1)S(1)} %get-tuple-element.23), channel_id=1, source_target_pairs={{1,9},{2,18},{3,11},{4,20},{5,13},{6,22},{7,15},{8,24},{9,1},{10,2... | collective-permute-start | bytes 417800 | tf_op jit(solution)/shard_map/ppermute | solution.py:147
  42.3 8.1 %collective-permute-start.14 = (s16[272,256]{1,0:T(8,128)(2,1)S(1)}, s16[272,256]{1,0:T(8,128)(2,1)S(1)}, u32[]{:S(2)}, u32[]{:S(2)}) collective-permute-start(s16[272,256]{1,0:T(8,128)(2,1)S(1)} %get-tuple-element.24), channel_id=1, source_target_pairs={{1,25},{2,26},{3,27},{4,28},{5,29},{6,30},{7,31},{8,16},{9,17},{10... | collective-permute-start | bytes 417800 | tf_op jit(solution)/shard_map/ppermute | solution.py:147
  50.5 3.7 %collective-permute-start.15 = (f32[4,256]{1,0:T(4,128)S(1)}, f32[4,256]{1,0:T(4,128)S(1)}, u32[]{:S(2)}, u32[]{:S(2)}) collective-permute-start(f32[4,256]{1,0:T(4,128)S(1)} %get-tuple-element.28.refs_2_), channel_id=1, source_target_pairs={{0,8},{8,0},{16,24},{24,16},{1,9},{9,1},{17,25},{25,17},{2,10},{10... | collective-permute-start | bytes 12296 | tf_op jit(solution)/shard_map/ppermute | solution.py:147
  51.9 3.6 %collective-permute-start.16 = (f32[4,256]{1,0:T(4,128)S(1)}, f32[4,256]{1,0:T(4,128)S(1)}, u32[]{:S(2)}, u32[]{:S(2)}) collective-permute-start(f32[4,256]{1,0:T(4,128)S(1)} %get-tuple-element.28.refs_2_), channel_id=1, source_target_pairs={{0,16},{8,24},{16,0},{24,8},{1,17},{9,25},{17,1},{25,9},{2,18},{10... | collective-permute-start | bytes 12296 | tf_op jit(solution)/shard_map/ppermute | solution.py:147
  52.0 4.5 %collective-permute-start.17 = (f32[4,256]{1,0:T(4,128)S(1)}, f32[4,256]{1,0:T(4,128)S(1)}, u32[]{:S(2)}, u32[]{:S(2)}) collective-permute-start(f32[4,256]{1,0:T(4,128)S(1)} %get-tuple-element.28.refs_2_), channel_id=1, source_target_pairs={{0,24},{8,16},{16,8},{24,0},{1,25},{9,17},{17,9},{25,1},{2,26},{10... | collective-permute-start | bytes 12296 | tf_op jit(solution)/shard_map/ppermute | solution.py:147
where the time goes:
time: 57.4 us; the launch traced here: 57.2 us
  waiting for transfers between devices  28.2 us (49%)
  starting transfers between devices  21.4 us (37%)
  Pallas kernels  4.98 us (9%)
  local copies, waits for them, and re-layouts  2.56 us (4%)
    ppermute x18, waiting for transfers between devices, move(): return lax.ppermute(x, axis, pairs[turn:] + pairs[:turn])  28.2 us
    ppermute x18, starting transfers between devices, move(): return lax.ppermute(x, axis, pairs[turn:] + pairs[:turn])  21.4 us
    pallas_call x2, Pallas kernels, shards(): pl.pallas_call(functools.partial(product_kernel, n_row, spans, half), out...  3.64 us
    unnamed x8, local copies, waits for them, and re-layouts  2.56 us
  transfers between devices with their start and end apart: 18, of which 9 were waited for; matrix products, arithmetic and copies ran while one was open for 0% of the time, Pallas kernels for 7%

commit v1 on v0

--- a/solution.py
+++ b/solution.py
@@ -17,15 +17,16 @@
 SMEM = pl.BlockSpec(memory_space=pltpu.SMEM)
 
 
-def stage_kernel(right_ref, out_ref, sems):
-    copies = [
-        pltpu.make_async_copy(right_ref.at[j], out_ref.at[j], sems.at[j])
-        for j in range(right_ref.shape[0])
-    ]
-    for copy in copies:
-        copy.start()
-    for copy in copies:
-        copy.wait()
+def stage_kernel(index_ref, count_ref, right_ref, out_ref):
+    column_blocks, slots = index_ref.shape
+    out_ref[...] = jnp.zeros_like(out_ref)
+    for j in range(column_blocks):
+        for q in range(slots):
+
+            def put(j=j, q=q):
+                out_ref[j, index_ref[j, q]] = right_ref[j, q]
+
+            pl.when(q < count_ref[j])(put)
 
 
 def far_half(half):
@@ -39,13 +40,13 @@
     return jnp.where(lax.axis_index("col") & 1 == 0, k, 3 - k)
 
 
-def product_kernel(n_row, spans, half, index_ref, count_ref, *refs):
+def product_kernel(n_row, spans, half, *refs):
     n_block = len(refs) - n_row - 3
     blocks, right_ref, own_ref = refs[:n_block], refs[n_block], refs[n_block + 1]
     sent_refs = refs[n_block + 2 : n_block + 1 + n_row]
     left, partial = refs[-2:]
-    column_blocks, slots, tile, _ = right_ref.shape
-    kept, height = left.shape[0] - 1, left.shape[1]
+    column_blocks, kept, tile, _ = right_ref.shape
+    height = left.shape[1]
     part = height // n_row // len(spans[0])
     row = lax.axis_index("row")
 
@@ -57,7 +58,7 @@
         return blocks[at] if a is None else blocks[at].at[a]
 
     if half is None:
-        left[:kept] = block_of(spans[0][0])[...]
+        left[...] = block_of(spans[0][0])[...]
     else:
         core, chip = lax.axis_index("col") & 1, lax.axis_index("col") >> 1
         ends = (chip == 0) | (chip == LINE - 1)
@@ -74,18 +75,16 @@
 
             def fill(role=role, k=k):
                 for at, span in enumerate(spans[role]):
-                    left[:kept, rows_of(chip ^ k, at), :] = block_of(span)[...]
+                    left[:, rows_of(chip ^ k, at), :] = block_of(span)[...]
 
             pl.when(wanted)(fill)
-    left[kept] = jnp.zeros(left.shape[1:], left.dtype)
     lines = lax.broadcasted_iota(jnp.int32, (CODE_ROWS, tile), 0)
     codes = jnp.zeros((CODE_ROWS, tile), jnp.int32)
     count = len(spans[0])
     for j in range(column_blocks):
         total = None
-        for q in range(slots):
-            picked = jnp.where(q < count_ref[j], index_ref[j, q], kept)
-            term = jnp.dot(left[picked], right_ref[j, q], preferred_element_type=jnp.float32)
+        for k in range(kept):
+            term = jnp.dot(left[k], right_ref[j, k], preferred_element_type=jnp.float32)
             total = term if total is None else total + term
         partial[...] = total
         top = jnp.max(total, axis=0, keepdims=True)
@@ -189,7 +188,7 @@
 
 def shards(n_row, n_col, left_tiles, right, right_index, right_count):
     windows, kept, _, tile = left_tiles.shape
-    column_blocks, slots = right.shape[:2]
+    column_blocks = right.shape[0]
     right_count = right_count.reshape(-1)
 
     if is_line(n_row, n_col):
@@ -203,13 +202,12 @@
 
     staged = pl.pallas_call(
         stage_kernel,
-        out_shape=jax.ShapeDtypeStruct(right.shape, right.dtype),
-        in_specs=[pl.BlockSpec(memory_space=pltpu.HBM)],
+        out_shape=jax.ShapeDtypeStruct((column_blocks, kept, tile, tile), right.dtype),
+        in_specs=[SMEM] * 2 + [VMEM],
         out_specs=VMEM,
-        scratch_shapes=[pltpu.SemaphoreType.DMA((column_blocks,))],
         compiler_params=limits(8),
         name="stage",
-    )(right)
+    )(right_index, right_count, right)
     exchanged = []
     for at, ((picked, half), (arrays, spans)) in enumerate(zip(chunks, gathered)):
         tall = height * len(picked)
@@ -218,20 +216,20 @@
             functools.partial(product_kernel, n_row, spans, half),
             out_shape=[jax.ShapeDtypeStruct((column_blocks, part, tile), jnp.float32)]
             + [jax.ShapeDtypeStruct((column_blocks * part + CODE_ROWS, tile), jnp.int16)] * (n_row - 1),
-            in_specs=[SMEM] * 2 + [VMEM] * (len(arrays) + 1),
+            in_specs=[VMEM] * (len(arrays) + 1),
             out_specs=[VMEM] * n_row,
             scratch_shapes=[
-                pltpu.VMEM((kept + 1, tall, tile), left_tiles.dtype),
+                pltpu.VMEM((kept, tall, tile), left_tiles.dtype),
                 pltpu.VMEM((tall, tile), jnp.float32),
             ],
             cost_estimate=pl.CostEstimate(
-                flops=2 * column_blocks * slots * tall * tile**2,
+                flops=2 * column_blocks * kept * tall * tile**2,
                 bytes_accessed=right.size * 2,
                 transcendentals=0,
             ),
             compiler_params=limits(16),
             name="product",
-        )(right_index, right_count, *arrays, staged)
+        )(*arrays, staged)
         got = [
             move(x, ("row", "col"), row_pairs(n_row, n_col, k, half), at)
             for k, x in enumerate(sent, 1)

time: 57.4 us -> 58.7 us (1.023)
  local copies, waits for them, and re-layouts: 2.56 us -> 3.23 us
    pallas_call x1, Pallas kernels: 0.25 us -> 1.11 us  [shards(): pl.pallas_call(stage_kernel, out_shape=jax.ShapeDtypeStruct((column_block...]
    unnamed x8, local copies, waits for them, and re-layouts: 2.56 us -> 3.23 us
  transfers between devices with their start and end apart: 18 -> 18, of which waited for: 9 -> 9; matrix products, arithmetic and copies ran while one was open for 0% -> 0% of each run, Pallas kernels for 7% -> 8%
where the time goes in v1:
time: 58.7 us; the launch traced here: 58.5 us
  waiting for transfers between devices  28.3 us (48%)
  starting transfers between devices  21.5 us (37%)
  Pallas kernels  5.33 us (9%)
  local copies, waits for them, and re-layouts  3.23 us (6%)
    ppermute x18, waiting for transfers between devices, move(): return lax.ppermute(x, axis, pairs[turn:] + pairs[:turn])  28.3 us
    ppermute x18, starting transfers between devices, move(): return lax.ppermute(x, axis, pairs[turn:] + pairs[:turn])  21.5 us
    unnamed x8, local copies, waits for them, and re-layouts  3.23 us
    pallas_call x2, Pallas kernels, shards(): pl.pallas_call(functools.partial(product_kernel, n_row, spans, half), out...  3.13 us
  transfers between devices with their start and end apart: 18, of which 9 were waited for; matrix products, arithmetic and copies ran while one was open for 0% of the time, Pallas kernels for 8%

profile of v1, /device:TPU:0, one launch (start us, length us, event | category | flops | bytes accessed | tf_op | source)
XLA Modules:
  0.0 58.5 jit_solution(12549074600071981463)
XLA Ops:
  0.0 4.1 %collective-permute-start.3 = (bf16[2,8,32,256]{3,2,1,0:T(8,128)(2,1)}, bf16[2,8,32,256]{3,2,1,0:T(8,128)(2,1)S(1)}, u32[]{:S(2)}, u32[]{:S(2)}) collective-permute-start(bf16[2,8,32,256]{3,2,1,0:T(8,128)(2,1)} %refs_0_.3), channel_id=1, source_target_pairs={{0,4},{1,7},{2,6},{3,5},{4,0},{5,3},{6,2},{7,1},{8,12},{9,15},{10,... | collective-permute-start | bytes 786440 | tf_op jit(solution)/shard_map/ppermute | solution.py:146
  4.1 0.6 collective-permute-start
  4.6 1.0 %collective-permute-start.1 = (bf16[2,8,32,256]{3,2,1,0:T(8,128)(2,1)}, bf16[2,8,32,256]{3,2,1,0:T(8,128)(2,1)S(1)}, u32[]{:S(2)}, u32[]{:S(2)}) collective-permute-start(bf16[2,8,32,256]{3,2,1,0:T(8,128)(2,1)} %refs_0_.3), channel_id=1, source_target_pairs={{0,2},{1,3},{2,0},{3,1},{4,6},{5,7},{6,4},{7,5},{8,10},{9,11},{10,... | collective-permute-start | bytes 786440 | tf_op jit(solution)/shard_map/ppermute | solution.py:146
  5.6 10.8 %collective-permute-done.3.refs_4_ = bf16[2,8,32,256]{3,2,1,0:T(8,128)(2,1)S(1)} collective-permute-done((bf16[2,8,32,256]{3,2,1,0:T(8,128)(2,1)}, bf16[2,8,32,256]{3,2,1,0:T(8,128)(2,1)S(1)}, u32[]{:S(2)}, u32[]{:S(2)}) %collective-permute-start.3) | collective-permute-done | bytes 262176 | tf_op jit(solution)/shard_map/ppermute | solution.py:146
  16.5 0.7 %collective-permute-start.10 = (bf16[2,8,32,256]{3,2,1,0:T(8,128)(2,1)S(1)}, bf16[2,8,32,256]{3,2,1,0:T(8,128)(2,1)S(1)}, u32[]{:S(2)}, u32[]{:S(2)}) collective-permute-start(bf16[2,8,32,256]{3,2,1,0:T(8,128)(2,1)S(1)} %collective-permute-done.3.refs_4_), channel_id=1, source_target_pairs={{2,1},{4,7},{10,9},{12,15},{18,17},{20,23},{26,25},{28,31}} | collective-permute-start | bytes 786440 | tf_op jit(solution)/shard_map/ppermute | solution.py:146
  17.1 2.1 %collective-permute-start.8 = (bf16[2,8,32,256]{3,2,1,0:T(8,128)(2,1)S(1)}, bf16[2,8,32,256]{3,2,1,0:T(8,128)(2,1)S(1)}, u32[]{:S(2)}, u32[]{:S(2)}) collective-permute-start(bf16[2,8,32,256]{3,2,1,0:T(8,128)(2,1)S(1)} %collective-permute-done.refs_1_), channel_id=1, source_target_pairs={{0,4},{1,1},{2,6},{3,5},{4,0},{5,3},{6,2},{7,7},{8,12},{9,9},{10,1... | collective-permute-start | bytes 786440 | tf_op jit(solution)/shard_map/ppermute | solution.py:146
  19.3 0.5 collective-permute-start.4
  19.8 1.7 %collective-permute-start.11 = (bf16[2,8,32,256]{3,2,1,0:T(8,128)(2,1)S(1)}, bf16[2,8,32,256]{3,2,1,0:T(8,128)(2,1)S(1)}, u32[]{:S(2)}, u32[]{:S(2)}) collective-permute-start(bf16[2,8,32,256]{3,2,1,0:T(8,128)(2,1)S(1)} %collective-permute-done.10.refs_6_), channel_id=1, source_target_pairs={{5,4},{6,7},{7,6},{0,1},{1,0},{2,3},{3,2},{4,5},{13,12},{14,15},{1... | collective-permute-start | bytes 786440 | tf_op jit(solution)/shard_map/ppermute | solution.py:146
  21.6 7.8 %collective-permute-done.8.refs_4_ = bf16[2,8,32,256]{3,2,1,0:T(8,128)(2,1)S(1)} collective-permute-done((bf16[2,8,32,256]{3,2,1,0:T(8,128)(2,1)S(1)}, bf16[2,8,32,256]{3,2,1,0:T(8,128)(2,1)S(1)}, u32[]{:S(2)}, u32[]{:S(2)}) %collective-permute-start.8) | collective-permute-done | bytes 262176 | tf_op jit(solution)/shard_map/ppermute | solution.py:146
  29.4 1.9 %copy-done = bf16[4,6,256,256]{3,2,1,0:T(8,128)(2,1)S(1)} copy-done((bf16[4,6,256,256]{3,2,1,0:T(8,128)(2,1)S(1)}, bf16[4,6,256,256]{3,2,1,0:T(8,128)(2,1)}, u32[]{:S(2)}) %copy-start) | copy-done | bytes 3145752
  31.3 0.7 %copy-done.2 = s32[4,6]{1,0:T(4,128)S(1)} copy-done((s32[4,6]{1,0:T(4,128)S(1)}, s32[4,6]{1,0:T(4,128)}, u32[]{:S(2)}) %copy-start.2) | copy-done | bytes 120
  32.0 0.7 %copy-done.3 = s32[4,1]{0,1:T(1,128)S(1)} copy-done((s32[4,1]{0,1:T(1,128)S(1)}, s32[4,1]{0,1:T(1,128)}, u32[]{:S(2)}) %copy-start.3) | copy-done | bytes 40
  32.6 1.1 %stage.1.refs_6_.refs_8_ = bf16[4,8,256,256]{3,2,1,0:T(8,128)(2,1)S(1)} custom-call(s32[4,6]{1,0:T(4,128)S(1)} %copy-done.2, s32[4]{0:T(128)S(1)} %bitcast.1, bf16[4,6,256,256]{3,2,1,0:T(8,128)(2,1)S(1)} %copy-done), custom_call_target="tpu_custom_call" | custom-call | tf_op jit(solution)/shard_map/stage/pallas_call | solution.py:203
  33.8 1.6 %product.2 = (f32[4,64,256]{2,1,0:T(8,128)S(1)}, s16[272,256]{1,0:T(8,128)(2,1)S(1)}, s16[272,256]{1,0:T(8,128)(2,1)S(1)}, s16[272,256]{1,0:T(8,128)(2,1)S(1)}) custom-call(bf16[2,8,32,256]{3,2,1,0:T(8,128)(2,1)S(1)} %copy-done.1, bf16[2,8,32,256]{3,2,1,0:T(8,128)(2,1)S(1)} %collective-permute-done.refs_1_, ...), custom_call_target="tpu_custom_call" | custom-call | flops 1073741824 | bytes 3145728 | tf_op jit(solution)/shard_map/product/pallas_call | solution.py:215
  35.3 1.4 %collective-permute-start.5 = (s16[272,256]{1,0:T(8,128)(2,1)S(1)}, s16[272,256]{1,0:T(8,128)(2,1)S(1)}, u32[]{:S(2)}, u32[]{:S(2)}) collective-permute-start(s16[272,256]{1,0:T(8,128)(2,1)S(1)} %get-tuple-element.17), channel_id=1, source_target_pairs={{0,8},{1,17},{2,10},{3,19},{4,12},{5,21},{6,14},{7,23},{8,0},{9,25... | collective-permute-start | bytes 417800 | tf_op jit(solution)/shard_map/ppermute | solution.py:146
  36.7 1.5 %collective-permute-start.6 = (s16[272,256]{1,0:T(8,128)(2,1)S(1)}, s16[272,256]{1,0:T(8,128)(2,1)S(1)}, u32[]{:S(2)}, u32[]{:S(2)}) collective-permute-start(s16[272,256]{1,0:T(8,128)(2,1)S(1)} %get-tuple-element.18), channel_id=1, source_target_pairs={{0,16},{1,9},{2,18},{3,11},{4,20},{5,13},{6,22},{7,15},{8,24},{9,1... | collective-permute-start | bytes 417800 | tf_op jit(solution)/shard_map/ppermute | solution.py:146
  38.2 0.7 %collective-permute-start.7 = (s16[272,256]{1,0:T(8,128)(2,1)S(1)}, s16[272,256]{1,0:T(8,128)(2,1)S(1)}, u32[]{:S(2)}, u32[]{:S(2)}) collective-permute-start(s16[272,256]{1,0:T(8,128)(2,1)S(1)} %get-tuple-element.19), channel_id=1, source_target_pairs={{0,24},{1,25},{2,26},{3,27},{4,28},{5,29},{6,30},{7,31},{8,16},{9,... | collective-permute-start | bytes 417800 | tf_op jit(solution)/shard_map/ppermute | solution.py:146
  38.9 1.6 %product.3 = (f32[4,64,256]{2,1,0:T(8,128)S(1)}, s16[272,256]{1,0:T(8,128)(2,1)S(1)}, s16[272,256]{1,0:T(8,128)(2,1)S(1)}, s16[272,256]{1,0:T(8,128)(2,1)S(1)}) custom-call(bf16[2,8,32,256]{3,2,1,0:T(8,128)(2,1)S(1)} %copy-done.1, bf16[2,8,32,256]{3,2,1,0:T(8,128)(2,1)S(1)} %collective-permute-done.refs_1_, ...), custom_call_target="tpu_custom_call" | custom-call | flops 1073741824 | bytes 3145728 | tf_op jit(solution)/shard_map/product/pallas_call | solution.py:215
  40.5 1.4 %collective-permute-start.12 = (s16[272,256]{1,0:T(8,128)(2,1)S(1)}, s16[272,256]{1,0:T(8,128)(2,1)S(1)}, u32[]{:S(2)}, u32[]{:S(2)}) collective-permute-start(s16[272,256]{1,0:T(8,128)(2,1)S(1)} %get-tuple-element.22), channel_id=1, source_target_pairs={{1,17},{2,10},{3,19},{4,12},{5,21},{6,14},{7,23},{8,0},{9,25},{10,... | collective-permute-start | bytes 417800 | tf_op jit(solution)/shard_map/ppermute | solution.py:146
  41.8 1.5 %collective-permute-start.13 = (s16[272,256]{1,0:T(8,128)(2,1)S(1)}, s16[272,256]{1,0:T(8,128)(2,1)S(1)}, u32[]{:S(2)}, u32[]{:S(2)}) collective-permute-start(s16[272,256]{1,0:T(8,128)(2,1)S(1)} %get-tuple-element.23), channel_id=1, source_target_pairs={{1,9},{2,18},{3,11},{4,20},{5,13},{6,22},{7,15},{8,24},{9,1},{10,2... | collective-permute-start | bytes 417800 | tf_op jit(solution)/shard_map/ppermute | solution.py:146
  43.3 0.8 %collective-permute-start.14 = (s16[272,256]{1,0:T(8,128)(2,1)S(1)}, s16[272,256]{1,0:T(8,128)(2,1)S(1)}, u32[]{:S(2)}, u32[]{:S(2)}) collective-permute-start(s16[272,256]{1,0:T(8,128)(2,1)S(1)} %get-tuple-element.24), channel_id=1, source_target_pairs={{1,25},{2,26},{3,27},{4,28},{5,29},{6,30},{7,31},{8,16},{9,17},{10... | collective-permute-start | bytes 417800 | tf_op jit(solution)/shard_map/ppermute | solution.py:146
  44.2 1.6 %collective-permute-done.7.refs_2_ = s16[272,256]{1,0:T(8,128)(2,1)S(1)} collective-permute-done((s16[272,256]{1,0:T(8,128)(2,1)S(1)}, s16[272,256]{1,0:T(8,128)(2,1)S(1)}, u32[]{:S(2)}, u32[]{:S(2)}) %collective-permute-start.7) | collective-permute-done | bytes 139296 | tf_op jit(solution)/shard_map/ppermute | solution.py:146
  45.7 0.2 reduce.2
  45.9 1.8 %collective-permute-done.12.refs_0_ = s16[272,256]{1,0:T(8,128)(2,1)S(1)} collective-permute-done((s16[272,256]{1,0:T(8,128)(2,1)S(1)}, s16[272,256]{1,0:T(8,128)(2,1)S(1)}, u32[]{:S(2)}, u32[]{:S(2)}) %collective-permute-start.12) | collective-permute-done | bytes 139296 | tf_op jit(solution)/shard_map/ppermute | solution.py:146
  47.7 0.9 %collective-permute-done.13.refs_1_ = s16[272,256]{1,0:T(8,128)(2,1)S(1)} collective-permute-done((s16[272,256]{1,0:T(8,128)(2,1)S(1)}, s16[272,256]{1,0:T(8,128)(2,1)S(1)}, u32[]{:S(2)}, u32[]{:S(2)}) %collective-permute-start.13) | collective-permute-done | bytes 139296 | tf_op jit(solution)/shard_map/ppermute | solution.py:146
  48.6 3.0 %collective-permute-done.14.refs_2_ = s16[272,256]{1,0:T(8,128)(2,1)S(1)} collective-permute-done((s16[272,256]{1,0:T(8,128)(2,1)S(1)}, s16[272,256]{1,0:T(8,128)(2,1)S(1)}, u32[]{:S(2)}, u32[]{:S(2)}) %collective-permute-start.14) | collective-permute-done | bytes 139296 | tf_op jit(solution)/shard_map/ppermute | solution.py:146
  51.7 0.2 reduce.3
  51.8 1.3 %collective-permute-start.15 = (f32[4,256]{1,0:T(4,128)S(1)}, f32[4,256]{1,0:T(4,128)S(1)}, u32[]{:S(2)}, u32[]{:S(2)}) collective-permute-start(f32[4,256]{1,0:T(4,128)S(1)} %get-tuple-element.28.refs_2_), channel_id=1, source_target_pairs={{0,8},{8,0},{16,24},{24,16},{1,9},{9,1},{17,25},{25,17},{2,10},{10... | collective-permute-start | bytes 12296 | tf_op jit(solution)/shard_map/ppermute | solution.py:146
  53.2 2.2 %collective-permute-start.17 = (f32[4,256]{1,0:T(4,128)S(1)}, f32[4,256]{1,0:T(4,128)S(1)}, u32[]{:S(2)}, u32[]{:S(2)}) collective-permute-start(f32[4,256]{1,0:T(4,128)S(1)} %get-tuple-element.28.refs_2_), channel_id=1, source_target_pairs={{0,24},{8,16},{16,8},{24,0},{1,25},{9,17},{17,9},{25,1},{2,26},{10... | collective-permute-start | bytes 12296 | tf_op jit(solution)/shard_map/ppermute | solution.py:146
  55.5 1.3 %collective-permute-done.16.refs_4_ = f32[4,256]{1,0:T(4,128)S(1)} collective-permute-done((f32[4,256]{1,0:T(4,128)S(1)}, f32[4,256]{1,0:T(4,128)S(1)}, u32[]{:S(2)}, u32[]{:S(2)}) %collective-permute-start.16) | collective-permute-done | bytes 4128 | tf_op jit(solution)/shard_map/ppermute | solution.py:146
  56.8 1.0 %collective-permute-done.17.refs_5_ = f32[4,256]{1,0:T(4,128)S(1)} collective-permute-done((f32[4,256]{1,0:T(4,128)S(1)}, f32[4,256]{1,0:T(4,128)S(1)}, u32[]{:S(2)}, u32[]{:S(2)}) %collective-permute-start.17) | collective-permute-done | bytes 4128 | tf_op jit(solution)/shard_map/ppermute | solution.py:146
  57.7 0.7 %scale.1 = bf16[2,4,64,256]{3,2,1,0:T(8,128)(2,1)} custom-call(f32[4,64,256]{2,1,0:T(8,128)S(1)} %get-tuple-element.21.refs_0_, f32[4,64,256]{2,1,0:T(8,128)S(1)} %get-tuple-element.27.refs_1_, f32[4,256]{1,0:T(4,128)S(1)} %get-tuple-element.28.refs_2_, f32[4,256]{1,0:T(4,128)S(1)} %collective-permute-done.15.refs_3_, ...), custom_call_target="tpu_custom_call" | custom-call | tf_op jit(solution)/shard_map/scale/pallas_call | solution.py:253
  (18 shorter events, 0.3 us)
Async XLA Ops:
  0.0 16.5 %collective-permute-start.3 = (bf16[2,8,32,256]{3,2,1,0:T(8,128)(2,1)}, bf16[2,8,32,256]{3,2,1,0:T(8,128)(2,1)S(1)}, u32[]{:S(2)}, u32[]{:S(2)}) collective-permute-start(bf16[2,8,32,256]{3,2,1,0:T(8,128)(2,1)} %refs_0_.3), channel_id=1, source_target_pairs={{0,4},{1,7},{2,6},{3,5},{4,0},{5,3},{6,2},{7,1},{8,12},{9,15},{10,... | collective-permute-start | bytes 786440 | tf_op jit(solution)/shard_map/ppermute | solution.py:146
  4.1 13.1 %collective-permute-start = (bf16[2,8,32,256]{3,2,1,0:T(8,128)(2,1)}, bf16[2,8,32,256]{3,2,1,0:T(8,128)(2,1)S(1)}, u32[]{:S(2)}, u32[]{:S(2)}) collective-permute-start(bf16[2,8,32,256]{3,2,1,0:T(8,128)(2,1)} %refs_0_.3), channel_id=1, source_target_pairs={{1,0},{2,3},{3,2},{4,5},{5,4},{6,7},{7,6},{0,1},{9,8},{10,11},{11,... | collective-permute-start | bytes 786440 | tf_op jit(solution)/shard_map/ppermute | solution.py:146
  4.6 14.6 %collective-permute-start.1 = (bf16[2,8,32,256]{3,2,1,0:T(8,128)(2,1)}, bf16[2,8,32,256]{3,2,1,0:T(8,128)(2,1)S(1)}, u32[]{:S(2)}, u32[]{:S(2)}) collective-permute-start(bf16[2,8,32,256]{3,2,1,0:T(8,128)(2,1)} %refs_0_.3), channel_id=1, source_target_pairs={{0,2},{1,3},{2,0},{3,1},{4,6},{5,7},{6,4},{7,5},{8,10},{9,11},{10,... | collective-permute-start | bytes 786440 | tf_op jit(solution)/shard_map/ppermute | solution.py:146
  16.5 3.4 %collective-permute-start.10 = (bf16[2,8,32,256]{3,2,1,0:T(8,128)(2,1)S(1)}, bf16[2,8,32,256]{3,2,1,0:T(8,128)(2,1)S(1)}, u32[]{:S(2)}, u32[]{:S(2)}) collective-permute-start(bf16[2,8,32,256]{3,2,1,0:T(8,128)(2,1)S(1)} %collective-permute-done.3.refs_4_), channel_id=1, source_target_pairs={{2,1},{4,7},{10,9},{12,15},{18,17},{20,23},{26,25},{28,31}} | collective-permute-start | bytes 786440 | tf_op jit(solution)/shard_map/ppermute | solution.py:146
  17.1 12.2 %collective-permute-start.8 = (bf16[2,8,32,256]{3,2,1,0:T(8,128)(2,1)S(1)}, bf16[2,8,32,256]{3,2,1,0:T(8,128)(2,1)S(1)}, u32[]{:S(2)}, u32[]{:S(2)}) collective-permute-start(bf16[2,8,32,256]{3,2,1,0:T(8,128)(2,1)S(1)} %collective-permute-done.refs_1_), channel_id=1, source_target_pairs={{0,4},{1,1},{2,6},{3,5},{4,0},{5,3},{6,2},{7,7},{8,12},{9,9},{10,1... | collective-permute-start | bytes 786440 | tf_op jit(solution)/shard_map/ppermute | solution.py:146
  19.3 14.5 %collective-permute-start.2 = (bf16[2,8,32,256]{3,2,1,0:T(8,128)(2,1)S(1)}, bf16[2,8,32,256]{3,2,1,0:T(8,128)(2,1)S(1)}, u32[]{:S(2)}, u32[]{:S(2)}) collective-permute-start(bf16[2,8,32,256]{3,2,1,0:T(8,128)(2,1)S(1)} %collective-permute-done.1.refs_2_), channel_id=1, source_target_pairs={{2,3},{3,2},{4,5},{5,4},{6,7},{7,6},{0,1},{1,0},{10,11},{11,10},{1... | collective-permute-start | bytes 786440 | tf_op jit(solution)/shard_map/ppermute | solution.py:146
  19.3 14.4 %collective-permute-start.4 = (bf16[2,8,32,256]{3,2,1,0:T(8,128)(2,1)S(1)}, bf16[2,8,32,256]{3,2,1,0:T(8,128)(2,1)S(1)}, u32[]{:S(2)}, u32[]{:S(2)}) collective-permute-start(bf16[2,8,32,256]{3,2,1,0:T(8,128)(2,1)S(1)} %collective-permute-done.3.refs_4_), channel_id=1, source_target_pairs={{3,2},{4,5},{5,4},{6,7},{7,6},{0,1},{1,0},{2,3},{11,10},{12,13},{1... | collective-permute-start | bytes 786440 | tf_op jit(solution)/shard_map/ppermute | solution.py:146
  19.8 19.1 %collective-permute-start.11 = (bf16[2,8,32,256]{3,2,1,0:T(8,128)(2,1)S(1)}, bf16[2,8,32,256]{3,2,1,0:T(8,128)(2,1)S(1)}, u32[]{:S(2)}, u32[]{:S(2)}) collective-permute-start(bf16[2,8,32,256]{3,2,1,0:T(8,128)(2,1)S(1)} %collective-permute-done.10.refs_6_), channel_id=1, source_target_pairs={{5,4},{6,7},{7,6},{0,1},{1,0},{2,3},{3,2},{4,5},{13,12},{14,15},{1... | collective-permute-start | bytes 786440 | tf_op jit(solution)/shard_map/ppermute | solution.py:146
  29.4 9.5 %collective-permute-start.9 = (bf16[2,8,32,256]{3,2,1,0:T(8,128)(2,1)S(1)}, bf16[2,8,32,256]{3,2,1,0:T(8,128)(2,1)S(1)}, u32[]{:S(2)}, u32[]{:S(2)}) collective-permute-start(bf16[2,8,32,256]{3,2,1,0:T(8,128)(2,1)S(1)} %collective-permute-done.8.refs_4_), channel_id=1, source_target_pairs={{4,5},{5,4},{6,7},{7,6},{0,1},{1,0},{2,3},{3,2},{12,13},{13,12},{1... | collective-permute-start | bytes 786440 | tf_op jit(solution)/shard_map/ppermute | solution.py:146
  29.4 1.9 %copy-start = (bf16[4,6,256,256]{3,2,1,0:T(8,128)(2,1)S(1)}, bf16[4,6,256,256]{3,2,1,0:T(8,128)(2,1)}, u32[]{:S(2)}) copy-start(bf16[4,6,256,256]{3,2,1,0:T(8,128)(2,1)} %right_ref.1) | copy-start | bytes 9437188
  31.3 0.7 %copy-start.2 = (s32[4,6]{1,0:T(4,128)S(1)}, s32[4,6]{1,0:T(4,128)}, u32[]{:S(2)}) copy-start(s32[4,6]{1,0:T(4,128)} %index_ref.1) | copy-start | bytes 292
  32.0 0.7 %copy-start.3 = (s32[4,1]{0,1:T(1,128)S(1)}, s32[4,1]{0,1:T(1,128)}, u32[]{:S(2)}) copy-start(s32[4,1]{0,1:T(1,128)} %param.7) | copy-start | bytes 52
  32.6 1.1 %copy-start.1 = (bf16[2,8,32,256]{3,2,1,0:T(8,128)(2,1)S(1)}, bf16[2,8,32,256]{3,2,1,0:T(8,128)(2,1)}, u32[]{:S(2)}) copy-start(bf16[2,8,32,256]{3,2,1,0:T(8,128)(2,1)} %refs_0_.3) | copy-start | bytes 786436
  35.3 8.0 %collective-permute-start.5 = (s16[272,256]{1,0:T(8,128)(2,1)S(1)}, s16[272,256]{1,0:T(8,128)(2,1)S(1)}, u32[]{:S(2)}, u32[]{:S(2)}) collective-permute-start(s16[272,256]{1,0:T(8,128)(2,1)S(1)} %get-tuple-element.17), channel_id=1, source_target_pairs={{0,8},{1,17},{2,10},{3,19},{4,12},{5,21},{6,14},{7,23},{8,0},{9,25... | collective-permute-start | bytes 417800 | tf_op jit(solution)/shard_map/ppermute | solution.py:146
  36.7 7.5 %collective-permute-start.6 = (s16[272,256]{1,0:T(8,128)(2,1)S(1)}, s16[272,256]{1,0:T(8,128)(2,1)S(1)}, u32[]{:S(2)}, u32[]{:S(2)}) collective-permute-start(s16[272,256]{1,0:T(8,128)(2,1)S(1)} %get-tuple-element.18), channel_id=1, source_target_pairs={{0,16},{1,9},{2,18},{3,11},{4,20},{5,13},{6,22},{7,15},{8,24},{9,1... | collective-permute-start | bytes 417800 | tf_op jit(solution)/shard_map/ppermute | solution.py:146
  38.2 7.6 %collective-permute-start.7 = (s16[272,256]{1,0:T(8,128)(2,1)S(1)}, s16[272,256]{1,0:T(8,128)(2,1)S(1)}, u32[]{:S(2)}, u32[]{:S(2)}) collective-permute-start(s16[272,256]{1,0:T(8,128)(2,1)S(1)} %get-tuple-element.19), channel_id=1, source_target_pairs={{0,24},{1,25},{2,26},{3,27},{4,28},{5,29},{6,30},{7,31},{8,16},{9,... | collective-permute-start | bytes 417800 | tf_op jit(solution)/shard_map/ppermute | solution.py:146
  40.5 7.3 %collective-permute-start.12 = (s16[272,256]{1,0:T(8,128)(2,1)S(1)}, s16[272,256]{1,0:T(8,128)(2,1)S(1)}, u32[]{:S(2)}, u32[]{:S(2)}) collective-permute-start(s16[272,256]{1,0:T(8,128)(2,1)S(1)} %get-tuple-element.22), channel_id=1, source_target_pairs={{1,17},{2,10},{3,19},{4,12},{5,21},{6,14},{7,23},{8,0},{9,25},{10,... | collective-permute-start | bytes 417800 | tf_op jit(solution)/shard_map/ppermute | solution.py:146
  41.8 6.8 %collective-permute-start.13 = (s16[272,256]{1,0:T(8,128)(2,1)S(1)}, s16[272,256]{1,0:T(8,128)(2,1)S(1)}, u32[]{:S(2)}, u32[]{:S(2)}) collective-permute-start(s16[272,256]{1,0:T(8,128)(2,1)S(1)} %get-tuple-element.23), channel_id=1, source_target_pairs={{1,9},{2,18},{3,11},{4,20},{5,13},{6,22},{7,15},{8,24},{9,1},{10,2... | collective-permute-start | bytes 417800 | tf_op jit(solution)/shard_map/ppermute | solution.py:146
  43.3 8.3 %collective-permute-start.14 = (s16[272,256]{1,0:T(8,128)(2,1)S(1)}, s16[272,256]{1,0:T(8,128)(2,1)S(1)}, u32[]{:S(2)}, u32[]{:S(2)}) collective-permute-start(s16[272,256]{1,0:T(8,128)(2,1)S(1)} %get-tuple-element.24), channel_id=1, source_target_pairs={{1,25},{2,26},{3,27},{4,28},{5,29},{6,30},{7,31},{8,16},{9,17},{10... | collective-permute-start | bytes 417800 | tf_op jit(solution)/shard_map/ppermute | solution.py:146
  51.8 3.7 %collective-permute-start.15 = (f32[4,256]{1,0:T(4,128)S(1)}, f32[4,256]{1,0:T(4,128)S(1)}, u32[]{:S(2)}, u32[]{:S(2)}) collective-permute-start(f32[4,256]{1,0:T(4,128)S(1)} %get-tuple-element.28.refs_2_), channel_id=1, source_target_pairs={{0,8},{8,0},{16,24},{24,16},{1,9},{9,1},{17,25},{25,17},{2,10},{10... | collective-permute-start | bytes 12296 | tf_op jit(solution)/shard_map/ppermute | solution.py:146
  53.2 3.6 %collective-permute-start.16 = (f32[4,256]{1,0:T(4,128)S(1)}, f32[4,256]{1,0:T(4,128)S(1)}, u32[]{:S(2)}, u32[]{:S(2)}) collective-permute-start(f32[4,256]{1,0:T(4,128)S(1)} %get-tuple-element.28.refs_2_), channel_id=1, source_target_pairs={{0,16},{8,24},{16,0},{24,8},{1,17},{9,25},{17,1},{25,9},{2,18},{10... | collective-permute-start | bytes 12296 | tf_op jit(solution)/shard_map/ppermute | solution.py:146
  53.2 4.5 %collective-permute-start.17 = (f32[4,256]{1,0:T(4,128)S(1)}, f32[4,256]{1,0:T(4,128)S(1)}, u32[]{:S(2)}, u32[]{:S(2)}) collective-permute-start(f32[4,256]{1,0:T(4,128)S(1)} %get-tuple-element.28.refs_2_), channel_id=1, source_target_pairs={{0,24},{8,16},{16,8},{24,0},{1,25},{9,17},{17,9},{25,1},{2,26},{10... | collective-permute-start | bytes 12296 | tf_op jit(solution)/shard_map/ppermute | solution.py:146

commit v2 on v1

--- a/solution.py
+++ b/solution.py
@@ -10,7 +10,7 @@
 LEVELS = 65280.0
 OFFSET = 32640
 LOG_STEPS = 256.0
-CODE_ROWS = 16
+CODE_ROWS = 8
 LINE = 4
 
 VMEM = pl.BlockSpec(memory_space=pltpu.VMEM)
@@ -174,9 +174,9 @@
     other = move(pair, "col", inner)
     relay = move(own, "col", [(2, 1), (n_col - 4, n_col - 1)])
     near_beside = move(beside, "col", swap, 2)
-    near_own = move(own, "col", swap, 3)
+    near_own = move(own, "col", swap, 2)
     near_other = move(other, "col", swap, 4)
-    near_relay = move(relay, "col", swap, 5)
+    near_relay = move(relay, "col", swap, 4)
     base = [left_tiles, pair, beside, near_beside]
     chunks, gathered = [], []
     for half, more in enumerate(([own, near_own], [other, near_other, relay, near_relay])):

time: 58.7 us -> 58.4 us (level)
  no operation moved by 1% of the time
where the time goes in v2:
time: 58.4 us; the launch traced here: 58.2 us
  waiting for transfers between devices  28.1 us (48%)
  starting transfers between devices  21.4 us (37%)
  Pallas kernels  5.33 us (9%)
  local copies, waits for them, and re-layouts  3.23 us (6%)
    ppermute x18, waiting for transfers between devices, move(): return lax.ppermute(x, axis, pairs[turn:] + pairs[:turn])  28.1 us
    ppermute x18, starting transfers between devices, move(): return lax.ppermute(x, axis, pairs[turn:] + pairs[:turn])  21.4 us
    unnamed x8, local copies, waits for them, and re-layouts  3.23 us
    pallas_call x2, Pallas kernels, shards(): pl.pallas_call(functools.partial(product_kernel, n_row, spans, half), out...  3.12 us
  transfers between devices with their start and end apart: 18, of which 9 were waited for; matrix products, arithmetic and copies ran while one was open for 0% of the time, Pallas kernels for 8%

profile of v2, /device:TPU:0, one launch (start us, length us, event | category | flops | bytes accessed | tf_op | source)
XLA Modules:
  0.0 58.2 jit_solution(5228990026666446139)
XLA Ops:
  0.0 4.1 %collective-permute-start.3 = (bf16[2,8,32,256]{3,2,1,0:T(8,128)(2,1)}, bf16[2,8,32,256]{3,2,1,0:T(8,128)(2,1)S(1)}, u32[]{:S(2)}, u32[]{:S(2)}) collective-permute-start(bf16[2,8,32,256]{3,2,1,0:T(8,128)(2,1)} %refs_0_.3), channel_id=1, source_target_pairs={{0,4},{1,7},{2,6},{3,5},{4,0},{5,3},{6,2},{7,1},{8,12},{9,15},{10,... | collective-permute-start | bytes 786440 | tf_op jit(solution)/shard_map/ppermute | solution.py:146
  4.1 0.6 collective-permute-start
  4.6 1.0 %collective-permute-start.1 = (bf16[2,8,32,256]{3,2,1,0:T(8,128)(2,1)}, bf16[2,8,32,256]{3,2,1,0:T(8,128)(2,1)S(1)}, u32[]{:S(2)}, u32[]{:S(2)}) collective-permute-start(bf16[2,8,32,256]{3,2,1,0:T(8,128)(2,1)} %refs_0_.3), channel_id=1, source_target_pairs={{0,2},{1,3},{2,0},{3,1},{4,6},{5,7},{6,4},{7,5},{8,10},{9,11},{10,... | collective-permute-start | bytes 786440 | tf_op jit(solution)/shard_map/ppermute | solution.py:146
  5.6 10.8 %collective-permute-done.3.refs_4_ = bf16[2,8,32,256]{3,2,1,0:T(8,128)(2,1)S(1)} collective-permute-done((bf16[2,8,32,256]{3,2,1,0:T(8,128)(2,1)}, bf16[2,8,32,256]{3,2,1,0:T(8,128)(2,1)S(1)}, u32[]{:S(2)}, u32[]{:S(2)}) %collective-permute-start.3) | collective-permute-done | bytes 262176 | tf_op jit(solution)/shard_map/ppermute | solution.py:146
  16.5 0.7 %collective-permute-start.10 = (bf16[2,8,32,256]{3,2,1,0:T(8,128)(2,1)S(1)}, bf16[2,8,32,256]{3,2,1,0:T(8,128)(2,1)S(1)}, u32[]{:S(2)}, u32[]{:S(2)}) collective-permute-start(bf16[2,8,32,256]{3,2,1,0:T(8,128)(2,1)S(1)} %collective-permute-done.3.refs_4_), channel_id=1, source_target_pairs={{2,1},{4,7},{10,9},{12,15},{18,17},{20,23},{26,25},{28,31}} | collective-permute-start | bytes 786440 | tf_op jit(solution)/shard_map/ppermute | solution.py:146
  17.1 2.1 %collective-permute-start.8 = (bf16[2,8,32,256]{3,2,1,0:T(8,128)(2,1)S(1)}, bf16[2,8,32,256]{3,2,1,0:T(8,128)(2,1)S(1)}, u32[]{:S(2)}, u32[]{:S(2)}) collective-permute-start(bf16[2,8,32,256]{3,2,1,0:T(8,128)(2,1)S(1)} %collective-permute-done.refs_1_), channel_id=1, source_target_pairs={{0,4},{1,1},{2,6},{3,5},{4,0},{5,3},{6,2},{7,7},{8,12},{9,9},{10,1... | collective-permute-start | bytes 786440 | tf_op jit(solution)/shard_map/ppermute | solution.py:146
  19.3 0.5 collective-permute-start.4
  19.8 1.7 %collective-permute-start.11 = (bf16[2,8,32,256]{3,2,1,0:T(8,128)(2,1)S(1)}, bf16[2,8,32,256]{3,2,1,0:T(8,128)(2,1)S(1)}, u32[]{:S(2)}, u32[]{:S(2)}) collective-permute-start(bf16[2,8,32,256]{3,2,1,0:T(8,128)(2,1)S(1)} %collective-permute-done.10.refs_6_), channel_id=1, source_target_pairs={{4,5},{5,4},{6,7},{7,6},{0,1},{1,0},{2,3},{3,2},{12,13},{13,12},{1... | collective-permute-start | bytes 786440 | tf_op jit(solution)/shard_map/ppermute | solution.py:146
  21.6 7.8 %collective-permute-done.8.refs_4_ = bf16[2,8,32,256]{3,2,1,0:T(8,128)(2,1)S(1)} collective-permute-done((bf16[2,8,32,256]{3,2,1,0:T(8,128)(2,1)S(1)}, bf16[2,8,32,256]{3,2,1,0:T(8,128)(2,1)S(1)}, u32[]{:S(2)}, u32[]{:S(2)}) %collective-permute-start.8) | collective-permute-done | bytes 262176 | tf_op jit(solution)/shard_map/ppermute | solution.py:146
  29.4 1.9 %copy-done = bf16[4,6,256,256]{3,2,1,0:T(8,128)(2,1)S(1)} copy-done((bf16[4,6,256,256]{3,2,1,0:T(8,128)(2,1)S(1)}, bf16[4,6,256,256]{3,2,1,0:T(8,128)(2,1)}, u32[]{:S(2)}) %copy-start) | copy-done | bytes 3145752
  31.3 0.7 %copy-done.2 = s32[4,6]{1,0:T(4,128)S(1)} copy-done((s32[4,6]{1,0:T(4,128)S(1)}, s32[4,6]{1,0:T(4,128)}, u32[]{:S(2)}) %copy-start.2) | copy-done | bytes 120
  32.0 0.7 %copy-done.3 = s32[4,1]{0,1:T(1,128)S(1)} copy-done((s32[4,1]{0,1:T(1,128)S(1)}, s32[4,1]{0,1:T(1,128)}, u32[]{:S(2)}) %copy-start.3) | copy-done | bytes 40
  32.6 1.1 %stage.1.refs_6_.refs_8_ = bf16[4,8,256,256]{3,2,1,0:T(8,128)(2,1)S(1)} custom-call(s32[4,6]{1,0:T(4,128)S(1)} %copy-done.2, s32[4]{0:T(128)S(1)} %bitcast.1, bf16[4,6,256,256]{3,2,1,0:T(8,128)(2,1)S(1)} %copy-done), custom_call_target="tpu_custom_call" | custom-call | tf_op jit(solution)/shard_map/stage/pallas_call | solution.py:203
  33.8 1.6 %product.2 = (f32[4,64,256]{2,1,0:T(8,128)S(1)}, s16[264,256]{1,0:T(8,128)(2,1)S(1)}, s16[264,256]{1,0:T(8,128)(2,1)S(1)}, s16[264,256]{1,0:T(8,128)(2,1)S(1)}) custom-call(bf16[2,8,32,256]{3,2,1,0:T(8,128)(2,1)S(1)} %copy-done.1, bf16[2,8,32,256]{3,2,1,0:T(8,128)(2,1)S(1)} %collective-permute-done.refs_1_, ...), custom_call_target="tpu_custom_call" | custom-call | flops 1073741824 | bytes 3145728 | tf_op jit(solution)/shard_map/product/pallas_call | solution.py:215
  35.3 1.4 %collective-permute-start.5 = (s16[264,256]{1,0:T(8,128)(2,1)S(1)}, s16[264,256]{1,0:T(8,128)(2,1)S(1)}, u32[]{:S(2)}, u32[]{:S(2)}) collective-permute-start(s16[264,256]{1,0:T(8,128)(2,1)S(1)} %get-tuple-element.17), channel_id=1, source_target_pairs={{0,8},{1,17},{2,10},{3,19},{4,12},{5,21},{6,14},{7,23},{8,0},{9,25... | collective-permute-start | bytes 405512 | tf_op jit(solution)/shard_map/ppermute | solution.py:146
  36.7 1.5 %collective-permute-start.6 = (s16[264,256]{1,0:T(8,128)(2,1)S(1)}, s16[264,256]{1,0:T(8,128)(2,1)S(1)}, u32[]{:S(2)}, u32[]{:S(2)}) collective-permute-start(s16[264,256]{1,0:T(8,128)(2,1)S(1)} %get-tuple-element.18), channel_id=1, source_target_pairs={{0,16},{1,9},{2,18},{3,11},{4,20},{5,13},{6,22},{7,15},{8,24},{9,1... | collective-permute-start | bytes 405512 | tf_op jit(solution)/shard_map/ppermute | solution.py:146
  38.2 0.7 %collective-permute-start.7 = (s16[264,256]{1,0:T(8,128)(2,1)S(1)}, s16[264,256]{1,0:T(8,128)(2,1)S(1)}, u32[]{:S(2)}, u32[]{:S(2)}) collective-permute-start(s16[264,256]{1,0:T(8,128)(2,1)S(1)} %get-tuple-element.19), channel_id=1, source_target_pairs={{0,24},{1,25},{2,26},{3,27},{4,28},{5,29},{6,30},{7,31},{8,16},{9,... | collective-permute-start | bytes 405512 | tf_op jit(solution)/shard_map/ppermute | solution.py:146
  38.9 1.6 %product.3 = (f32[4,64,256]{2,1,0:T(8,128)S(1)}, s16[264,256]{1,0:T(8,128)(2,1)S(1)}, s16[264,256]{1,0:T(8,128)(2,1)S(1)}, s16[264,256]{1,0:T(8,128)(2,1)S(1)}) custom-call(bf16[2,8,32,256]{3,2,1,0:T(8,128)(2,1)S(1)} %copy-done.1, bf16[2,8,32,256]{3,2,1,0:T(8,128)(2,1)S(1)} %collective-permute-done.refs_1_, ...), custom_call_target="tpu_custom_call" | custom-call | flops 1073741824 | bytes 3145728 | tf_op jit(solution)/shard_map/product/pallas_call | solution.py:215
  40.5 1.4 %collective-permute-start.12 = (s16[264,256]{1,0:T(8,128)(2,1)S(1)}, s16[264,256]{1,0:T(8,128)(2,1)S(1)}, u32[]{:S(2)}, u32[]{:S(2)}) collective-permute-start(s16[264,256]{1,0:T(8,128)(2,1)S(1)} %get-tuple-element.22), channel_id=1, source_target_pairs={{1,17},{2,10},{3,19},{4,12},{5,21},{6,14},{7,23},{8,0},{9,25},{10,... | collective-permute-start | bytes 405512 | tf_op jit(solution)/shard_map/ppermute | solution.py:146
  41.8 1.5 %collective-permute-start.13 = (s16[264,256]{1,0:T(8,128)(2,1)S(1)}, s16[264,256]{1,0:T(8,128)(2,1)S(1)}, u32[]{:S(2)}, u32[]{:S(2)}) collective-permute-start(s16[264,256]{1,0:T(8,128)(2,1)S(1)} %get-tuple-element.23), channel_id=1, source_target_pairs={{1,9},{2,18},{3,11},{4,20},{5,13},{6,22},{7,15},{8,24},{9,1},{10,2... | collective-permute-start | bytes 405512 | tf_op jit(solution)/shard_map/ppermute | solution.py:146
  43.3 0.8 %collective-permute-start.14 = (s16[264,256]{1,0:T(8,128)(2,1)S(1)}, s16[264,256]{1,0:T(8,128)(2,1)S(1)}, u32[]{:S(2)}, u32[]{:S(2)}) collective-permute-start(s16[264,256]{1,0:T(8,128)(2,1)S(1)} %get-tuple-element.24), channel_id=1, source_target_pairs={{1,25},{2,26},{3,27},{4,28},{5,29},{6,30},{7,31},{8,16},{9,17},{10... | collective-permute-start | bytes 405512 | tf_op jit(solution)/shard_map/ppermute | solution.py:146
  44.1 1.5 %collective-permute-done.7.refs_2_ = s16[264,256]{1,0:T(8,128)(2,1)S(1)} collective-permute-done((s16[264,256]{1,0:T(8,128)(2,1)S(1)}, s16[264,256]{1,0:T(8,128)(2,1)S(1)}, u32[]{:S(2)}, u32[]{:S(2)}) %collective-permute-start.7) | collective-permute-done | bytes 135200 | tf_op jit(solution)/shard_map/ppermute | solution.py:146
  45.6 0.2 reduce.2
  45.8 1.8 %collective-permute-done.12.refs_0_ = s16[264,256]{1,0:T(8,128)(2,1)S(1)} collective-permute-done((s16[264,256]{1,0:T(8,128)(2,1)S(1)}, s16[264,256]{1,0:T(8,128)(2,1)S(1)}, u32[]{:S(2)}, u32[]{:S(2)}) %collective-permute-start.12) | collective-permute-done | bytes 135200 | tf_op jit(solution)/shard_map/ppermute | solution.py:146
  47.6 0.8 %collective-permute-done.13.refs_1_ = s16[264,256]{1,0:T(8,128)(2,1)S(1)} collective-permute-done((s16[264,256]{1,0:T(8,128)(2,1)S(1)}, s16[264,256]{1,0:T(8,128)(2,1)S(1)}, u32[]{:S(2)}, u32[]{:S(2)}) %collective-permute-start.13) | collective-permute-done | bytes 135200 | tf_op jit(solution)/shard_map/ppermute | solution.py:146
  48.4 2.9 %collective-permute-done.14.refs_2_ = s16[264,256]{1,0:T(8,128)(2,1)S(1)} collective-permute-done((s16[264,256]{1,0:T(8,128)(2,1)S(1)}, s16[264,256]{1,0:T(8,128)(2,1)S(1)}, u32[]{:S(2)}, u32[]{:S(2)}) %collective-permute-start.14) | collective-permute-done | bytes 135200 | tf_op jit(solution)/shard_map/ppermute | solution.py:146
  51.3 0.2 reduce.3
  51.5 1.3 %collective-permute-start.15 = (f32[4,256]{1,0:T(4,128)S(1)}, f32[4,256]{1,0:T(4,128)S(1)}, u32[]{:S(2)}, u32[]{:S(2)}) collective-permute-start(f32[4,256]{1,0:T(4,128)S(1)} %get-tuple-element.28.refs_2_), channel_id=1, source_target_pairs={{0,8},{8,0},{16,24},{24,16},{1,9},{9,1},{17,25},{25,17},{2,10},{10... | collective-permute-start | bytes 12296 | tf_op jit(solution)/shard_map/ppermute | solution.py:146
  52.9 2.1 %collective-permute-start.17 = (f32[4,256]{1,0:T(4,128)S(1)}, f32[4,256]{1,0:T(4,128)S(1)}, u32[]{:S(2)}, u32[]{:S(2)}) collective-permute-start(f32[4,256]{1,0:T(4,128)S(1)} %get-tuple-element.28.refs_2_), channel_id=1, source_target_pairs={{0,24},{8,16},{16,8},{24,0},{1,25},{9,17},{17,9},{25,1},{2,26},{10... | collective-permute-start | bytes 12296 | tf_op jit(solution)/shard_map/ppermute | solution.py:146
  55.2 1.2 %collective-permute-done.16.refs_4_ = f32[4,256]{1,0:T(4,128)S(1)} collective-permute-done((f32[4,256]{1,0:T(4,128)S(1)}, f32[4,256]{1,0:T(4,128)S(1)}, u32[]{:S(2)}, u32[]{:S(2)}) %collective-permute-start.16) | collective-permute-done | bytes 4128 | tf_op jit(solution)/shard_map/ppermute | solution.py:146
  56.4 1.0 %collective-permute-done.17.refs_5_ = f32[4,256]{1,0:T(4,128)S(1)} collective-permute-done((f32[4,256]{1,0:T(4,128)S(1)}, f32[4,256]{1,0:T(4,128)S(1)}, u32[]{:S(2)}, u32[]{:S(2)}) %collective-permute-start.17) | collective-permute-done | bytes 4128 | tf_op jit(solution)/shard_map/ppermute | solution.py:146
  57.4 0.7 %scale.1 = bf16[2,4,64,256]{3,2,1,0:T(8,128)(2,1)} custom-call(f32[4,64,256]{2,1,0:T(8,128)S(1)} %get-tuple-element.21.refs_0_, f32[4,64,256]{2,1,0:T(8,128)S(1)} %get-tuple-element.27.refs_1_, f32[4,256]{1,0:T(4,128)S(1)} %get-tuple-element.28.refs_2_, f32[4,256]{1,0:T(4,128)S(1)} %collective-permute-done.15.refs_3_, ...), custom_call_target="tpu_custom_call" | custom-call | tf_op jit(solution)/shard_map/scale/pallas_call | solution.py:253
  (18 shorter events, 0.3 us)
Async XLA Ops:
  0.0 16.5 %collective-permute-start.3 = (bf16[2,8,32,256]{3,2,1,0:T(8,128)(2,1)}, bf16[2,8,32,256]{3,2,1,0:T(8,128)(2,1)S(1)}, u32[]{:S(2)}, u32[]{:S(2)}) collective-permute-start(bf16[2,8,32,256]{3,2,1,0:T(8,128)(2,1)} %refs_0_.3), channel_id=1, source_target_pairs={{0,4},{1,7},{2,6},{3,5},{4,0},{5,3},{6,2},{7,1},{8,12},{9,15},{10,... | collective-permute-start | bytes 786440 | tf_op jit(solution)/shard_map/ppermute | solution.py:146
  4.1 13.1 %collective-permute-start = (bf16[2,8,32,256]{3,2,1,0:T(8,128)(2,1)}, bf16[2,8,32,256]{3,2,1,0:T(8,128)(2,1)S(1)}, u32[]{:S(2)}, u32[]{:S(2)}) collective-permute-start(bf16[2,8,32,256]{3,2,1,0:T(8,128)(2,1)} %refs_0_.3), channel_id=1, source_target_pairs={{1,0},{2,3},{3,2},{4,5},{5,4},{6,7},{7,6},{0,1},{9,8},{10,11},{11,... | collective-permute-start | bytes 786440 | tf_op jit(solution)/shard_map/ppermute | solution.py:146
  4.6 14.6 %collective-permute-start.1 = (bf16[2,8,32,256]{3,2,1,0:T(8,128)(2,1)}, bf16[2,8,32,256]{3,2,1,0:T(8,128)(2,1)S(1)}, u32[]{:S(2)}, u32[]{:S(2)}) collective-permute-start(bf16[2,8,32,256]{3,2,1,0:T(8,128)(2,1)} %refs_0_.3), channel_id=1, source_target_pairs={{0,2},{1,3},{2,0},{3,1},{4,6},{5,7},{6,4},{7,5},{8,10},{9,11},{10,... | collective-permute-start | bytes 786440 | tf_op jit(solution)/shard_map/ppermute | solution.py:146
  16.5 3.4 %collective-permute-start.10 = (bf16[2,8,32,256]{3,2,1,0:T(8,128)(2,1)S(1)}, bf16[2,8,32,256]{3,2,1,0:T(8,128)(2,1)S(1)}, u32[]{:S(2)}, u32[]{:S(2)}) collective-permute-start(bf16[2,8,32,256]{3,2,1,0:T(8,128)(2,1)S(1)} %collective-permute-done.3.refs_4_), channel_id=1, source_target_pairs={{2,1},{4,7},{10,9},{12,15},{18,17},{20,23},{26,25},{28,31}} | collective-permute-start | bytes 786440 | tf_op jit(solution)/shard_map/ppermute | solution.py:146
  17.1 12.2 %collective-permute-start.8 = (bf16[2,8,32,256]{3,2,1,0:T(8,128)(2,1)S(1)}, bf16[2,8,32,256]{3,2,1,0:T(8,128)(2,1)S(1)}, u32[]{:S(2)}, u32[]{:S(2)}) collective-permute-start(bf16[2,8,32,256]{3,2,1,0:T(8,128)(2,1)S(1)} %collective-permute-done.refs_1_), channel_id=1, source_target_pairs={{0,4},{1,1},{2,6},{3,5},{4,0},{5,3},{6,2},{7,7},{8,12},{9,9},{10,1... | collective-permute-start | bytes 786440 | tf_op jit(solution)/shard_map/ppermute | solution.py:146
  19.3 14.5 %collective-permute-start.2 = (bf16[2,8,32,256]{3,2,1,0:T(8,128)(2,1)S(1)}, bf16[2,8,32,256]{3,2,1,0:T(8,128)(2,1)S(1)}, u32[]{:S(2)}, u32[]{:S(2)}) collective-permute-start(bf16[2,8,32,256]{3,2,1,0:T(8,128)(2,1)S(1)} %collective-permute-done.1.refs_2_), channel_id=1, source_target_pairs={{2,3},{3,2},{4,5},{5,4},{6,7},{7,6},{0,1},{1,0},{10,11},{11,10},{1... | collective-permute-start | bytes 786440 | tf_op jit(solution)/shard_map/ppermute | solution.py:146
  19.3 14.4 %collective-permute-start.4 = (bf16[2,8,32,256]{3,2,1,0:T(8,128)(2,1)S(1)}, bf16[2,8,32,256]{3,2,1,0:T(8,128)(2,1)S(1)}, u32[]{:S(2)}, u32[]{:S(2)}) collective-permute-start(bf16[2,8,32,256]{3,2,1,0:T(8,128)(2,1)S(1)} %collective-permute-done.3.refs_4_), channel_id=1, source_target_pairs={{2,3},{3,2},{4,5},{5,4},{6,7},{7,6},{0,1},{1,0},{10,11},{11,10},{1... | collective-permute-start | bytes 786440 | tf_op jit(solution)/shard_map/ppermute | solution.py:146
  19.8 19.1 %collective-permute-start.11 = (bf16[2,8,32,256]{3,2,1,0:T(8,128)(2,1)S(1)}, bf16[2,8,32,256]{3,2,1,0:T(8,128)(2,1)S(1)}, u32[]{:S(2)}, u32[]{:S(2)}) collective-permute-start(bf16[2,8,32,256]{3,2,1,0:T(8,128)(2,1)S(1)} %collective-permute-done.10.refs_6_), channel_id=1, source_target_pairs={{4,5},{5,4},{6,7},{7,6},{0,1},{1,0},{2,3},{3,2},{12,13},{13,12},{1... | collective-permute-start | bytes 786440 | tf_op jit(solution)/shard_map/ppermute | solution.py:146
  29.4 9.5 %collective-permute-start.9 = (bf16[2,8,32,256]{3,2,1,0:T(8,128)(2,1)S(1)}, bf16[2,8,32,256]{3,2,1,0:T(8,128)(2,1)S(1)}, u32[]{:S(2)}, u32[]{:S(2)}) collective-permute-start(bf16[2,8,32,256]{3,2,1,0:T(8,128)(2,1)S(1)} %collective-permute-done.8.refs_4_), channel_id=1, source_target_pairs={{4,5},{5,4},{6,7},{7,6},{0,1},{1,0},{2,3},{3,2},{12,13},{13,12},{1... | collective-permute-start | bytes 786440 | tf_op jit(solution)/shard_map/ppermute | solution.py:146
  29.4 1.9 %copy-start = (bf16[4,6,256,256]{3,2,1,0:T(8,128)(2,1)S(1)}, bf16[4,6,256,256]{3,2,1,0:T(8,128)(2,1)}, u32[]{:S(2)}) copy-start(bf16[4,6,256,256]{3,2,1,0:T(8,128)(2,1)} %right_ref.1) | copy-start | bytes 9437188
  31.3 0.7 %copy-start.2 = (s32[4,6]{1,0:T(4,128)S(1)}, s32[4,6]{1,0:T(4,128)}, u32[]{:S(2)}) copy-start(s32[4,6]{1,0:T(4,128)} %index_ref.1) | copy-start | bytes 292
  32.0 0.7 %copy-start.3 = (s32[4,1]{0,1:T(1,128)S(1)}, s32[4,1]{0,1:T(1,128)}, u32[]{:S(2)}) copy-start(s32[4,1]{0,1:T(1,128)} %param.7) | copy-start | bytes 52
  32.6 1.1 %copy-start.1 = (bf16[2,8,32,256]{3,2,1,0:T(8,128)(2,1)S(1)}, bf16[2,8,32,256]{3,2,1,0:T(8,128)(2,1)}, u32[]{:S(2)}) copy-start(bf16[2,8,32,256]{3,2,1,0:T(8,128)(2,1)} %refs_0_.3) | copy-start | bytes 786436
  35.3 8.0 %collective-permute-start.5 = (s16[264,256]{1,0:T(8,128)(2,1)S(1)}, s16[264,256]{1,0:T(8,128)(2,1)S(1)}, u32[]{:S(2)}, u32[]{:S(2)}) collective-permute-start(s16[264,256]{1,0:T(8,128)(2,1)S(1)} %get-tuple-element.17), channel_id=1, source_target_pairs={{0,8},{1,17},{2,10},{3,19},{4,12},{5,21},{6,14},{7,23},{8,0},{9,25... | collective-permute-start | bytes 405512 | tf_op jit(solution)/shard_map/ppermute | solution.py:146
  36.7 7.4 %collective-permute-start.6 = (s16[264,256]{1,0:T(8,128)(2,1)S(1)}, s16[264,256]{1,0:T(8,128)(2,1)S(1)}, u32[]{:S(2)}, u32[]{:S(2)}) collective-permute-start(s16[264,256]{1,0:T(8,128)(2,1)S(1)} %get-tuple-element.18), channel_id=1, source_target_pairs={{0,16},{1,9},{2,18},{3,11},{4,20},{5,13},{6,22},{7,15},{8,24},{9,1... | collective-permute-start | bytes 405512 | tf_op jit(solution)/shard_map/ppermute | solution.py:146
  38.2 7.4 %collective-permute-start.7 = (s16[264,256]{1,0:T(8,128)(2,1)S(1)}, s16[264,256]{1,0:T(8,128)(2,1)S(1)}, u32[]{:S(2)}, u32[]{:S(2)}) collective-permute-start(s16[264,256]{1,0:T(8,128)(2,1)S(1)} %get-tuple-element.19), channel_id=1, source_target_pairs={{0,24},{1,25},{2,26},{3,27},{4,28},{5,29},{6,30},{7,31},{8,16},{9,... | collective-permute-start | bytes 405512 | tf_op jit(solution)/shard_map/ppermute | solution.py:146
  40.5 7.1 %collective-permute-start.12 = (s16[264,256]{1,0:T(8,128)(2,1)S(1)}, s16[264,256]{1,0:T(8,128)(2,1)S(1)}, u32[]{:S(2)}, u32[]{:S(2)}) collective-permute-start(s16[264,256]{1,0:T(8,128)(2,1)S(1)} %get-tuple-element.22), channel_id=1, source_target_pairs={{1,17},{2,10},{3,19},{4,12},{5,21},{6,14},{7,23},{8,0},{9,25},{10,... | collective-permute-start | bytes 405512 | tf_op jit(solution)/shard_map/ppermute | solution.py:146
  41.8 6.5 %collective-permute-start.13 = (s16[264,256]{1,0:T(8,128)(2,1)S(1)}, s16[264,256]{1,0:T(8,128)(2,1)S(1)}, u32[]{:S(2)}, u32[]{:S(2)}) collective-permute-start(s16[264,256]{1,0:T(8,128)(2,1)S(1)} %get-tuple-element.23), channel_id=1, source_target_pairs={{1,9},{2,18},{3,11},{4,20},{5,13},{6,22},{7,15},{8,24},{9,1},{10,2... | collective-permute-start | bytes 405512 | tf_op jit(solution)/shard_map/ppermute | solution.py:146
  43.3 8.0 %collective-permute-start.14 = (s16[264,256]{1,0:T(8,128)(2,1)S(1)}, s16[264,256]{1,0:T(8,128)(2,1)S(1)}, u32[]{:S(2)}, u32[]{:S(2)}) collective-permute-start(s16[264,256]{1,0:T(8,128)(2,1)S(1)} %get-tuple-element.24), channel_id=1, source_target_pairs={{1,25},{2,26},{3,27},{4,28},{5,29},{6,30},{7,31},{8,16},{9,17},{10... | collective-permute-start | bytes 405512 | tf_op jit(solution)/shard_map/ppermute | solution.py:146
  51.5 3.7 %collective-permute-start.15 = (f32[4,256]{1,0:T(4,128)S(1)}, f32[4,256]{1,0:T(4,128)S(1)}, u32[]{:S(2)}, u32[]{:S(2)}) collective-permute-start(f32[4,256]{1,0:T(4,128)S(1)} %get-tuple-element.28.refs_2_), channel_id=1, source_target_pairs={{0,8},{8,0},{16,24},{24,16},{1,9},{9,1},{17,25},{25,17},{2,10},{10... | collective-permute-start | bytes 12296 | tf_op jit(solution)/shard_map/ppermute | solution.py:146
  52.8 3.6 %collective-permute-start.16 = (f32[4,256]{1,0:T(4,128)S(1)}, f32[4,256]{1,0:T(4,128)S(1)}, u32[]{:S(2)}, u32[]{:S(2)}) collective-permute-start(f32[4,256]{1,0:T(4,128)S(1)} %get-tuple-element.28.refs_2_), channel_id=1, source_target_pairs={{0,16},{8,24},{16,0},{24,8},{1,17},{9,25},{17,1},{25,9},{2,18},{10... | collective-permute-start | bytes 12296 | tf_op jit(solution)/shard_map/ppermute | solution.py:146
  52.9 4.5 %collective-permute-start.17 = (f32[4,256]{1,0:T(4,128)S(1)}, f32[4,256]{1,0:T(4,128)S(1)}, u32[]{:S(2)}, u32[]{:S(2)}) collective-permute-start(f32[4,256]{1,0:T(4,128)S(1)} %get-tuple-element.28.refs_2_), channel_id=1, source_target_pairs={{0,24},{8,16},{16,8},{24,0},{1,25},{9,17},{17,9},{25,1},{2,26},{10... | collective-permute-start | bytes 12296 | tf_op jit(solution)/shard_map/ppermute | solution.py:146
